TPU v7x, 32 devices: a whole 2x2x4 slice. The times are simulated.
32 devices in a mesh: tm: 8 (over z, y), obs: 4 (over x, core).
Axes of the slice: x: 2, y: 2, z: 4, core: 2. Of those that a mesh axis runs over, the one named last changes fastest.
Arguments:
- trajectory: bfloat16 [8, 64, 256, 128], P('tm', 'obs'), may hold values from -6 to 6
- weights: bfloat16 [1024, 128, 256], P(('tm', 'obs')), may hold values from -0.375 to 0.375
- observed: bfloat16 [1024, 128, 128], P(('tm', 'obs')), may hold values from -9 to 9
- window: int32 [1024, 1], P(('tm', 'obs')), may hold values from 0 to 7; in each aligned block of 32 rows (0 to 31, 32 to 63, ...) at most 4 rows name the same one
- block: int32 [1024], P(('tm', 'obs')), may hold values from 0 to 15
- counts: int32 [1024], P(('tm', 'obs')), may hold values from 32 to 128, as said below
- flags: int32 [1024, 128], P(('tm', 'obs')), may hold values 0 or 1
- inv_error: float32 [128], replicated, may hold values from 0.5 to 2
Outputs:
- departures: bfloat16 [1024, 128, 128], P(('tm', 'obs'))
- window_bias: float32 [8, 128], P('tm')
- window_chi: float32 [8, 128], P('tm')
Inputs may be any that keep to these rules, and one draw needn't show every extreme that they name: Among the 32 groups of one device, no sub-window is named by more than 4. `counts`: among the 32 groups of one device, one has all 128 slots live.
All inputs are finite; a program needn't handle non-finite values. No bound on the sum of `flags` on one device may be relied on, other than what follows from the above.
Results may differ from a plain program's by a relative error of at most 0.001.
Values may be sent and summed in bfloat16 or wider, within the bound.
No kernel may reach another device: no remote copies, remote signals or barrier semaphores. Data moves between devices by JAX's collectives and lax.ppermute only.
A program may use at most 64 MiB of HBM per device.

v0:
```python
import jax
import jax.numpy as jnp
from jax import lax
from jax.experimental import pallas as pl
from jax.experimental.pallas import tpu as pltpu
from jax.sharding import PartitionSpec as P


GCAP = 4
STEP = 8


ANY = pl.BlockSpec(memory_space=pl.ANY)
SMEM = pl.BlockSpec(memory_space=pltpu.SMEM)


def swap(x, axis, bits):
    size = lax.axis_size(axis)
    return lax.ppermute(x, axis, [(i, i ^ bits) for i in range(size)])


def gather_rows(ids, slab, pieces, first, rows):
    width = slab.shape[2]

    def body(ids_ref, slab_ref, *refs):
        outs, sems = refs[:pieces], refs[pieces]
        copies = []
        for piece in range(pieces):
            for k in range(GCAP):
                copy = pltpu.make_async_copy(
                    slab_ref.at[ids_ref[piece, k], pl.ds(first, rows)],
                    outs[piece].at[k],
                    sems.at[piece * GCAP + k],
                )
                copy.start()
                copies.append(copy)
        for copy in copies:
            copy.wait()

    return pl.pallas_call(
        body,
        in_specs=[SMEM, ANY],
        out_specs=[pl.BlockSpec(memory_space=pltpu.VMEM)] * pieces,
        out_shape=[jax.ShapeDtypeStruct((GCAP, rows, width), slab.dtype)] * pieces,
        scratch_shapes=[pltpu.SemaphoreType.DMA((pieces * GCAP,))],
    )(ids, slab)


def departures_kernel(
    slab, mirror, near, far_low, far_high, slot_of, win_of, own_ids, mirror_ids, weights, observed, used_t, inv_error,
    kept_rows, low,
):
    groups, slots, cells = weights.shape
    levels = observed.shape[2]
    windows = kept_rows.shape[0]
    half = windows // 2
    n_near, n_low, n_high = len(near), len(far_low), len(far_high)
    opposite = windows - 2
    n_sems = 2 * GCAP + n_near + n_low + n_high

    def body(slot_ref, win_ref, own_ref, mir_ref, w_ref, y_ref, u_ref, inv_ref, kept_ref, slab_ref, mirror_ref, *refs):
        near_refs = refs[:n_near]
        low_refs = refs[n_near:n_near + n_low]
        high_refs = refs[n_near + n_low:n_near + n_low + n_high]
        out_ref, sum_ref, x_ref, sems = refs[n_near + n_low + n_high:]
        step = pl.program_id(0)

        @pl.when(step == 0)
        def _():
            copies = []

            def add(src, dst):
                copy = pltpu.make_async_copy(src, dst, sems.at[len(copies)])
                copy.start()
                copies.append(copy)

            for k in range(GCAP):
                add(slab_ref.at[own_ref[k]], x_ref.at[k])
                add(mirror_ref.at[mir_ref[k]], x_ref.at[opposite * GCAP + k, pl.ds(0, low)])
            for j in range(1, half):
                add(near_refs[j - 1], x_ref.at[pl.ds(j * GCAP, GCAP)])
                add(low_refs[j - 1], x_ref.at[pl.ds((j ^ opposite) * GCAP, GCAP), pl.ds(0, low)])
            for j in range(half, windows):
                add(high_refs[j - half], x_ref.at[pl.ds(j * GCAP, GCAP), pl.ds(low, cells - low)])
            sum_ref[0] = jnp.zeros((windows, levels), jnp.float32)
            sum_ref[1] = jnp.zeros((windows, levels), jnp.float32)
            sum_ref[2] = kept_ref[...]
            for copy in copies:
                copy.wait()

        inv = inv_ref[...]
        for i in range(STEP):
            g = step * STEP + i
            x = x_ref[slot_ref[g]]
            hx = jnp.dot(w_ref[i], x, preferred_element_type=jnp.float32)
            dep = u_ref[0, :, i:i + 1] * (y_ref[i].astype(jnp.float32) - hx) * inv
            out_ref[i] = dep.astype(jnp.bfloat16)
            w = win_ref[g]
            sum_ref[0, pl.ds(w, 1), :] += jnp.sum(dep, 0, keepdims=True)
            sum_ref[1, pl.ds(w, 1), :] += jnp.sum(dep * dep, 0, keepdims=True)

    return pl.pallas_call(
        body,
        grid=(groups // STEP,),
        in_specs=[SMEM] * 4
        + [
            pl.BlockSpec((STEP, slots, cells), lambda s: (s, 0, 0)),
            pl.BlockSpec((STEP, slots, levels), lambda s: (s, 0, 0)),
            pl.BlockSpec((1, slots, STEP), lambda s: (s, 0, 0)),
            pl.BlockSpec((1, levels), lambda s: (0, 0)),
            pl.BlockSpec((windows, levels), lambda s: (0, 0)),
        ]
        + [ANY] * (2 + n_near + n_low + n_high),
        out_specs=[
            pl.BlockSpec((STEP, slots, levels), lambda s: (s, 0, 0)),
            pl.BlockSpec((3, windows, levels), lambda s: (0, 0, 0)),
        ],
        out_shape=[
            jax.ShapeDtypeStruct((groups, slots, levels), jnp.bfloat16),
            jax.ShapeDtypeStruct((3, windows, levels), jnp.float32),
        ],
        scratch_shapes=[
            pltpu.VMEM((windows * GCAP, cells, levels), slab.dtype),
            pltpu.SemaphoreType.DMA((n_sems,)),
        ],
    )(
        slot_of, win_of, own_ids, mirror_ids, weights, observed, used_t, inv_error[None, :], kept_rows,
        slab, mirror, *near, *far_low, *far_high,
    )


def body(trajectory, weights, observed, window, block, counts, flags, inv_error):
    groups, slots, cells = weights.shape
    levels = observed.shape[2]
    windows = lax.axis_size("tm")
    half = windows // 2
    opposite = windows - 2
    low = cells * 3 // 8 // 16 * 16
    me = lax.axis_index("tm")
    slab = trajectory[0]

    mirror = swap(slab[:, :low], "tm", opposite)

    win_of = window[:, 0]
    gid = jnp.arange(groups, dtype=jnp.int32)
    rank = jnp.sum(((win_of[:, None] == win_of[None, :]) & (gid[None, :] < gid[:, None])).astype(jnp.int32), 1)
    code = win_of * GCAP + rank
    wanted = jnp.sum(
        jnp.where(code[None, :] == jnp.arange(windows * GCAP, dtype=jnp.int32)[:, None], block[None, :], 0), 1
    ).reshape(windows, GCAP)
    across = wanted.reshape(2, half // 2, 2, GCAP)[::-1, ::-1].reshape(windows, GCAP)
    request = jnp.concatenate([wanted, across], 1)
    asked = lax.all_to_all(request, "tm", split_axis=0, concat_axis=0, tiled=True)
    by_xor = asked[jnp.arange(windows, dtype=jnp.int32) ^ me]

    send_high = gather_rows(by_xor[half:, :GCAP], slab, half, low, cells - low)
    far_high = [swap(send_high[j - half], "tm", j) for j in range(half, windows)]
    send_near = gather_rows(by_xor[1:half, :GCAP], slab, half - 1, 0, cells)
    near = [swap(send_near[j - 1], "tm", j) for j in range(1, half)]
    send_low = gather_rows(by_xor[1:half, GCAP:], mirror, half - 1, 0, low)
    far_low = [swap(send_low[j - 1], "tm", j) for j in range(1, half)]

    slot_ids = lax.broadcasted_iota(jnp.int32, (groups, slots), 1)
    used = jnp.where(slot_ids < counts[:, None], flags, 0).astype(jnp.float32)
    used_t = used.reshape(groups // STEP, STEP, slots).transpose(0, 2, 1)
    member = win_of[None, :] == jnp.arange(windows, dtype=jnp.int32)[:, None]
    kept = jnp.sum(jnp.where(member, jnp.sum(used, 1)[None, :], 0.0), 1)
    kept_rows = jnp.broadcast_to(kept[:, None], (windows, levels))

    slot_of = (win_of ^ me) * GCAP + rank
    departures, sums = departures_kernel(
        slab, mirror, near, far_low, far_high, slot_of, win_of, wanted[me], wanted[me ^ opposite], weights, observed,
        used_t, inv_error, kept_rows, low,
    )
    for axis in ("obs", "tm"):
        bits = 1
        while bits < lax.axis_size(axis):
            sums = sums + swap(sums, axis, bits)
            bits *= 2
    mine = lax.dynamic_slice_in_dim(sums, me, 1, 1)
    window_bias = mine[0] / jnp.sqrt(mine[2] + 1.0)
    window_chi = mine[1] / (mine[2] + 1.0)
    return (departures, window_bias, window_chi)


def solution(mesh):
    return jax.shard_map(
        body,
        mesh=mesh,
        in_specs=(
            P("tm", "obs", None, None),
            P(("tm", "obs"), None, None),
            P(("tm", "obs"), None, None),
            P(("tm", "obs"), None),
            P(("tm", "obs")),
            P(("tm", "obs")),
            P(("tm", "obs"), None),
            P(),
        ),
        out_specs=(P(("tm", "obs"), None, None), P("tm", None), P("tm", None)),
        check_vma=False,
    )
```

profile of v0, /device:TPU:0, one launch (start us, length us, event | category | flops | bytes accessed | tf_op | source)
XLA Modules:
  0.0 96.6 jit_solution(2188240592503326507)
XLA Ops:
  1.6 1.2 %multiply_add_fusion = (s32[32]{0:T(128)S(1)}, s32[32]{0:T(128)}) fusion(s32[32]{0:T(128)S(1)} %convert_reduce_fusion.1, s32[32,1]{0,1:T(1,128)} %param.11, s32[]{:T(128)S(6)} %axis_index.15), kind=kLoop, calls=%fused_computation.25 | loop fusion | flops 160 | bytes 516 | tf_op jit(solution)/shard_map/add | solution.py:147
  4.4 7.3 %all-to-all-start = ((s32[8,1,8]{2,1,0:T(1,128)}), s32[8,1,8]{2,1,0:T(1,128)S(1)}, u32[]{:S(2)}, u32[]{:S(2)}) async-start(s32[8,1,8]{2,1,0:T(1,128)} %bitcast.9), calls=%async_computation | async-start | bytes 8192 | tf_op jit(solution)/shard_map/all_to_all | solution.py:153
  12.7 3.9 %collective-permute-start = (bf16[16,96,128]{2,1,0:T(8,128)(2,1)S(1)}, bf16[16,96,128]{2,1,0:T(8,128)(2,1)S(1)}, u32[]{:S(2)}, u32[]{:S(2)}) collective-permute-start(bf16[16,96,128]{2,1,0:T(8,128)(2,1)S(1)} %slice.31), channel_id=1, source_target_pairs={{0,24},{4,28},{8,16},{12,20},{16,8},{20,12},{24,0},{28,4},{1,25},{... | collective-permute-start | bytes 1179656 | tf_op jit(solution)/shard_map/ppermute | solution.py:19
  16.6 1.6 %all-to-all-done = s32[8,1,8]{2,1,0:T(1,128)S(1)} async-done(((s32[8,1,8]{2,1,0:T(1,128)}), s32[8,1,8]{2,1,0:T(1,128)S(1)}, u32[]{:S(2)}, u32[]{:S(2)}) %all-to-all-start) | async-done | bytes 288 | tf_op jit(solution)/shard_map/all_to_all | solution.py:153
  19.4 2.8 %shard_map.105 = (bf16[4,160,128]{2,1,0:T(8,128)(2,1)}, bf16[4,160,128]{2,1,0:T(8,128)(2,1)}, bf16[4,160,128]{2,1,0:T(8,128)(2,1)}, bf16[4,160,128]{2,1,0:T(8,128)(2,1)}) custom-call(s32[4,4]{1,0:T(4,128)} %slice.25.ids_ref, bf16[16,256,128]{2,1,0:T(8,128)(2,1)} %bitcast.24), custom_call_target="tpu_custom_call" | custom-call | tf_op jit(solution)/shard_map/pallas_call | solution.py:40
  22.7 2.5 %collective-permute-start.8 = (bf16[4,160,128]{2,1,0:T(8,128)(2,1)}, bf16[4,160,128]{2,1,0:T(8,128)(2,1)S(1)}, u32[]{:S(2)}, u32[]{:S(2)}) collective-permute-start(bf16[4,160,128]{2,1,0:T(8,128)(2,1)} %get-tuple-element.22), channel_id=1, source_target_pairs={{0,20},{4,16},{8,28},{12,24},{16,4},{20,0},{24,12},{28,8},{1,21},{... | collective-permute-start | bytes 491528 | tf_op jit(solution)/shard_map/ppermute | solution.py:19
  25.8 2.8 %shard_map.103 = (bf16[4,256,128]{2,1,0:T(8,128)(2,1)}, bf16[4,256,128]{2,1,0:T(8,128)(2,1)}, bf16[4,256,128]{2,1,0:T(8,128)(2,1)}) custom-call(s32[3,4]{1,0:T(4,128)} %get-tuple-element.28.ids_ref, bf16[16,256,128]{2,1,0:T(8,128)(2,1)} %bitcast.25), custom_call_target="tpu_custom_call" | custom-call | tf_op jit(solution)/shard_map/pallas_call | solution.py:40
  28.6 1.5 %collective-permute-start.1 = (bf16[4,256,128]{2,1,0:T(8,128)(2,1)}, bf16[4,256,128]{2,1,0:T(8,128)(2,1)S(1)}, u32[]{:S(2)}, u32[]{:S(2)}) collective-permute-start(bf16[4,256,128]{2,1,0:T(8,128)(2,1)} %get-tuple-element.15), channel_id=1, source_target_pairs={{0,4},{4,0},{8,12},{12,8},{16,20},{20,16},{24,28},{28,24},{1,5},{5... | collective-permute-start | bytes 786440 | tf_op jit(solution)/shard_map/ppermute | solution.py:19
  30.7 17.1 %collective-permute-done.7.refs_6_ = bf16[4,160,128]{2,1,0:T(8,128)(2,1)S(1)} collective-permute-done((bf16[4,160,128]{2,1,0:T(8,128)(2,1)}, bf16[4,160,128]{2,1,0:T(8,128)(2,1)S(1)}, u32[]{:S(2)}, u32[]{:S(2)}) %collective-permute-start.7) | collective-permute-done | bytes 163872 | tf_op jit(solution)/shard_map/ppermute | solution.py:19
  47.7 4.2 %collective-permute-start.10 = (bf16[4,160,128]{2,1,0:T(8,128)(2,1)}, bf16[4,160,128]{2,1,0:T(8,128)(2,1)S(1)}, u32[]{:S(2)}, u32[]{:S(2)}) collective-permute-start(bf16[4,160,128]{2,1,0:T(8,128)(2,1)} %get-tuple-element.24), channel_id=1, source_target_pairs={{0,28},{4,24},{8,20},{12,16},{16,12},{20,8},{24,4},{28,0},{1,29},{... | collective-permute-start | bytes 491528 | tf_op jit(solution)/shard_map/ppermute | solution.py:19
  52.0 2.2 %collective-permute-done.8.refs_7_ = bf16[4,160,128]{2,1,0:T(8,128)(2,1)S(1)} collective-permute-done((bf16[4,160,128]{2,1,0:T(8,128)(2,1)}, bf16[4,160,128]{2,1,0:T(8,128)(2,1)S(1)}, u32[]{:S(2)}, u32[]{:S(2)}) %collective-permute-start.8) | collective-permute-done | bytes 163872 | tf_op jit(solution)/shard_map/ppermute | solution.py:19
  55.7 2.4 %shard_map.104 = (bf16[4,96,128]{2,1,0:T(8,128)(2,1)}, bf16[4,96,128]{2,1,0:T(8,128)(2,1)}, bf16[4,96,128]{2,1,0:T(8,128)(2,1)}) custom-call(s32[3,4]{1,0:T(4,128)} %get-tuple-element.27.ids_ref, bf16[16,96,128]{2,1,0:T(8,128)(2,1)} %copy-done), custom_call_target="tpu_custom_call" | custom-call | tf_op jit(solution)/shard_map/pallas_call | solution.py:40
  58.2 3.2 %collective-permute-start.4 = (bf16[4,96,128]{2,1,0:T(8,128)(2,1)}, bf16[4,96,128]{2,1,0:T(8,128)(2,1)S(1)}, u32[]{:S(2)}, u32[]{:S(2)}) collective-permute-start(bf16[4,96,128]{2,1,0:T(8,128)(2,1)} %get-tuple-element.18), channel_id=1, source_target_pairs={{0,4},{4,0},{8,12},{12,8},{16,20},{20,16},{24,28},{28,24},{1,5},{5... | collective-permute-start | bytes 294920 | tf_op jit(solution)/shard_map/ppermute | solution.py:19
  61.3 3.0 %collective-permute-start.5 = (bf16[4,96,128]{2,1,0:T(8,128)(2,1)}, bf16[4,96,128]{2,1,0:T(8,128)(2,1)S(1)}, u32[]{:S(2)}, u32[]{:S(2)}) collective-permute-start(bf16[4,96,128]{2,1,0:T(8,128)(2,1)} %get-tuple-element.19), channel_id=1, source_target_pairs={{0,8},{4,12},{8,0},{12,4},{16,24},{20,28},{24,16},{28,20},{1,9},{5... | collective-permute-start | bytes 294920 | tf_op jit(solution)/shard_map/ppermute | solution.py:19
  65.3 3.0 %collective-permute-done.3.refs_2_ = bf16[4,256,128]{2,1,0:T(8,128)(2,1)S(1)} collective-permute-done((bf16[4,256,128]{2,1,0:T(8,128)(2,1)}, bf16[4,256,128]{2,1,0:T(8,128)(2,1)S(1)}, u32[]{:S(2)}, u32[]{:S(2)}) %collective-permute-start.3) | collective-permute-done | bytes 262176 | tf_op jit(solution)/shard_map/ppermute | solution.py:19
  68.3 1.4 %collective-permute-done.5.refs_4_ = bf16[4,96,128]{2,1,0:T(8,128)(2,1)S(1)} collective-permute-done((bf16[4,96,128]{2,1,0:T(8,128)(2,1)}, bf16[4,96,128]{2,1,0:T(8,128)(2,1)S(1)}, u32[]{:S(2)}, u32[]{:S(2)}) %collective-permute-start.5) | collective-permute-done | bytes 98336 | tf_op jit(solution)/shard_map/ppermute | solution.py:19
  69.7 1.5 %collective-permute-done.6.refs_5_ = bf16[4,96,128]{2,1,0:T(8,128)(2,1)S(1)} collective-permute-done((bf16[4,96,128]{2,1,0:T(8,128)(2,1)}, bf16[4,96,128]{2,1,0:T(8,128)(2,1)S(1)}, u32[]{:S(2)}, u32[]{:S(2)}) %collective-permute-start.6) | collective-permute-done | bytes 98336 | tf_op jit(solution)/shard_map/ppermute | solution.py:19
  72.0 6.2 %shard_map.106 = (bf16[32,128,128]{2,1,0:T(8,128)(2,1)}, f32[3,8,128]{2,1,0:T(8,128)}) custom-call(s32[32]{0:T(128)} %get-tuple-element.34.slot_ref, s32[32]{0:T(128)} %bitcast.31, s32[4]{0:T(128)} %get-tuple-element.30.own_ref, s32[4]{0:T(128)} %get-tuple-element.29.mir_ref, bf16[32,128,256]{2,1,0:T(8,128)(2,1)} %w_ref.1, bf16[32,128,128]{2,1,0:T(8,128)(2,1)} %y_ref.1, ...), custom_call_target="tpu_custom_call" | custom-call | tf_op jit(solution)/shard_map/pallas_call | solution.py:102
  78.2 1.4 %collective-permute-done.11 = f32[3,8,128]{2,1,0:T(8,128)S(1)} collective-permute-done((f32[3,8,128]{2,1,0:T(8,128)}, f32[3,8,128]{2,1,0:T(8,128)S(1)}, u32[]{:S(2)}, u32[]{:S(2)}) %collective-permute-start.11) | collective-permute-done | bytes 12320 | tf_op jit(solution)/shard_map/ppermute | solution.py:19
  80.3 1.5 %collective-permute-start.12 = (f32[3,8,128]{2,1,0:T(8,128)S(1)}, f32[3,8,128]{2,1,0:T(8,128)S(1)}, u32[]{:S(2)}, u32[]{:S(2)}) collective-permute-start(f32[3,8,128]{2,1,0:T(8,128)S(1)} %add.64), channel_id=1, source_target_pairs={{0,2},{1,3},{2,0},{3,1},{4,6},{5,7},{6,4},{7,5},{8,10},{9,11},{10,... | collective-permute-start | bytes 36872 | tf_op jit(solution)/shard_map/ppermute | solution.py:19
  81.8 2.2 %collective-permute-done.12 = f32[3,8,128]{2,1,0:T(8,128)S(1)} collective-permute-done((f32[3,8,128]{2,1,0:T(8,128)S(1)}, f32[3,8,128]{2,1,0:T(8,128)S(1)}, u32[]{:S(2)}, u32[]{:S(2)}) %collective-permute-start.12) | collective-permute-done | bytes 12320 | tf_op jit(solution)/shard_map/ppermute | solution.py:19
  85.0 2.7 %collective-permute-done.13 = f32[3,8,128]{2,1,0:T(8,128)S(1)} collective-permute-done((f32[3,8,128]{2,1,0:T(8,128)S(1)}, f32[3,8,128]{2,1,0:T(8,128)S(1)}, u32[]{:S(2)}, u32[]{:S(2)}) %collective-permute-start.13) | collective-permute-done | bytes 12320 | tf_op jit(solution)/shard_map/ppermute | solution.py:19
  87.8 3.6 %collective-permute-done.14 = f32[3,8,128]{2,1,0:T(8,128)S(1)} collective-permute-done((f32[3,8,128]{2,1,0:T(8,128)S(1)}, f32[3,8,128]{2,1,0:T(8,128)S(1)}, u32[]{:S(2)}, u32[]{:S(2)}) %collective-permute-start.14) | collective-permute-done | bytes 12320 | tf_op jit(solution)/shard_map/ppermute | solution.py:19
  92.2 3.8 %collective-permute-done.15 = f32[3,8,128]{2,1,0:T(8,128)S(1)} collective-permute-done((f32[3,8,128]{2,1,0:T(8,128)S(1)}, f32[3,8,128]{2,1,0:T(8,128)S(1)}, u32[]{:S(2)}, u32[]{:S(2)}) %collective-permute-start.15) | collective-permute-done | bytes 12320 | tf_op jit(solution)/shard_map/ppermute | solution.py:19
  (67 shorter events, 12.7 us)
Async XLA Ops:
  0.6 55.0 %copy-start.13 = (s32[32,1]{0,1:T(1,128)S(1)}, s32[32,1]{0,1:T(1,128)}, u32[]{:S(2)}) copy-start(s32[32,1]{0,1:T(1,128)} %param.11) | copy-start | bytes 388
  0.6 29.5 %copy-start.11 = (s32[32,128]{1,0:T(8,128)S(1)}, s32[32,128]{1,0:T(8,128)}, u32[]{:S(2)}) copy-start(s32[32,128]{1,0:T(8,128)} %param.14) | copy-start | bytes 49156
  0.7 29.5 %copy-start.12 = (s32[32]{0:T(128)S(1)}, s32[32]{0:T(128)}, u32[]{:S(2)}) copy-start(s32[32]{0:T(128)} %param.13) | copy-start | bytes 388
  4.4 13.8 %all-to-all-start = ((s32[8,1,8]{2,1,0:T(1,128)}), s32[8,1,8]{2,1,0:T(1,128)S(1)}, u32[]{:S(2)}, u32[]{:S(2)}) async-start(s32[8,1,8]{2,1,0:T(1,128)} %bitcast.9), calls=%async_computation | async-start | bytes 8192 | tf_op jit(solution)/shard_map/all_to_all | solution.py:153
  12.7 41.5 %collective-permute-start = (bf16[16,96,128]{2,1,0:T(8,128)(2,1)S(1)}, bf16[16,96,128]{2,1,0:T(8,128)(2,1)S(1)}, u32[]{:S(2)}, u32[]{:S(2)}) collective-permute-start(bf16[16,96,128]{2,1,0:T(8,128)(2,1)S(1)} %slice.31), channel_id=1, source_target_pairs={{0,24},{4,28},{8,16},{12,20},{16,8},{20,12},{24,0},{28,4},{1,25},{... | collective-permute-start | bytes 1179656 | tf_op jit(solution)/shard_map/ppermute | solution.py:19
  22.1 25.6 %collective-permute-start.7 = (bf16[4,160,128]{2,1,0:T(8,128)(2,1)}, bf16[4,160,128]{2,1,0:T(8,128)(2,1)S(1)}, u32[]{:S(2)}, u32[]{:S(2)}) collective-permute-start(bf16[4,160,128]{2,1,0:T(8,128)(2,1)} %get-tuple-element.21), channel_id=1, source_target_pairs={{0,16},{4,20},{8,24},{12,28},{16,0},{20,4},{24,8},{28,12},{1,17},{... | collective-permute-start | bytes 491528 | tf_op jit(solution)/shard_map/ppermute | solution.py:19
  22.7 31.5 %collective-permute-start.8 = (bf16[4,160,128]{2,1,0:T(8,128)(2,1)}, bf16[4,160,128]{2,1,0:T(8,128)(2,1)S(1)}, u32[]{:S(2)}, u32[]{:S(2)}) collective-permute-start(bf16[4,160,128]{2,1,0:T(8,128)(2,1)} %get-tuple-element.22), channel_id=1, source_target_pairs={{0,20},{4,16},{8,28},{12,24},{16,4},{20,0},{24,12},{28,8},{1,21},{... | collective-permute-start | bytes 491528 | tf_op jit(solution)/shard_map/ppermute | solution.py:19
  28.6 35.7 %collective-permute-start.1 = (bf16[4,256,128]{2,1,0:T(8,128)(2,1)}, bf16[4,256,128]{2,1,0:T(8,128)(2,1)S(1)}, u32[]{:S(2)}, u32[]{:S(2)}) collective-permute-start(bf16[4,256,128]{2,1,0:T(8,128)(2,1)} %get-tuple-element.15), channel_id=1, source_target_pairs={{0,4},{4,0},{8,12},{12,8},{16,20},{20,16},{24,28},{28,24},{1,5},{5... | collective-permute-start | bytes 786440 | tf_op jit(solution)/shard_map/ppermute | solution.py:19
  30.2 27.9 %collective-permute-start.9 = (bf16[4,160,128]{2,1,0:T(8,128)(2,1)}, bf16[4,160,128]{2,1,0:T(8,128)(2,1)S(1)}, u32[]{:S(2)}, u32[]{:S(2)}) collective-permute-start(bf16[4,160,128]{2,1,0:T(8,128)(2,1)} %get-tuple-element.23), channel_id=1, source_target_pairs={{0,24},{4,28},{8,16},{12,20},{16,8},{20,12},{24,0},{28,4},{1,25},{... | collective-permute-start | bytes 491528 | tf_op jit(solution)/shard_map/ppermute | solution.py:19
  47.7 24.2 %copy-start.4 = (bf16[4,160,128]{2,1,0:T(8,128)(2,1)}, bf16[4,160,128]{2,1,0:T(8,128)(2,1)S(1)}, u32[]{:S(2)}) copy-start(bf16[4,160,128]{2,1,0:T(8,128)(2,1)S(1)} %collective-permute-done.7.refs_6_) | copy-start | bytes 491524
  47.7 13.6 %collective-permute-start.10 = (bf16[4,160,128]{2,1,0:T(8,128)(2,1)}, bf16[4,160,128]{2,1,0:T(8,128)(2,1)S(1)}, u32[]{:S(2)}, u32[]{:S(2)}) collective-permute-start(bf16[4,160,128]{2,1,0:T(8,128)(2,1)} %get-tuple-element.24), channel_id=1, source_target_pairs={{0,28},{4,24},{8,20},{12,16},{16,12},{20,8},{24,4},{28,0},{1,29},{... | collective-permute-start | bytes 491528 | tf_op jit(solution)/shard_map/ppermute | solution.py:19
  54.2 17.7 %copy-start.5 = (bf16[4,160,128]{2,1,0:T(8,128)(2,1)}, bf16[4,160,128]{2,1,0:T(8,128)(2,1)S(1)}, u32[]{:S(2)}) copy-start(bf16[4,160,128]{2,1,0:T(8,128)(2,1)S(1)} %collective-permute-done.8.refs_7_) | copy-start | bytes 491524
  54.2 11.1 %collective-permute-start.2 = (bf16[4,256,128]{2,1,0:T(8,128)(2,1)}, bf16[4,256,128]{2,1,0:T(8,128)(2,1)S(1)}, u32[]{:S(2)}, u32[]{:S(2)}) collective-permute-start(bf16[4,256,128]{2,1,0:T(8,128)(2,1)} %get-tuple-element.16), channel_id=1, source_target_pairs={{0,8},{4,12},{8,0},{12,4},{16,24},{20,28},{24,16},{28,20},{1,9},{5... | collective-permute-start | bytes 786440 | tf_op jit(solution)/shard_map/ppermute | solution.py:19
  54.2 14.1 %collective-permute-start.3 = (bf16[4,256,128]{2,1,0:T(8,128)(2,1)}, bf16[4,256,128]{2,1,0:T(8,128)(2,1)S(1)}, u32[]{:S(2)}, u32[]{:S(2)}) collective-permute-start(bf16[4,256,128]{2,1,0:T(8,128)(2,1)} %get-tuple-element.17), channel_id=1, source_target_pairs={{0,12},{4,8},{8,4},{12,0},{16,28},{20,24},{24,20},{28,16},{1,13},{... | collective-permute-start | bytes 786440 | tf_op jit(solution)/shard_map/ppermute | solution.py:19
  58.2 13.8 %copy-start.6 = (bf16[4,160,128]{2,1,0:T(8,128)(2,1)}, bf16[4,160,128]{2,1,0:T(8,128)(2,1)S(1)}, u32[]{:S(2)}) copy-start(bf16[4,160,128]{2,1,0:T(8,128)(2,1)S(1)} %collective-permute-done.9.refs_8_) | copy-start | bytes 491524
  58.2 10.1 %collective-permute-start.4 = (bf16[4,96,128]{2,1,0:T(8,128)(2,1)}, bf16[4,96,128]{2,1,0:T(8,128)(2,1)S(1)}, u32[]{:S(2)}, u32[]{:S(2)}) collective-permute-start(bf16[4,96,128]{2,1,0:T(8,128)(2,1)} %get-tuple-element.18), channel_id=1, source_target_pairs={{0,4},{4,0},{8,12},{12,8},{16,20},{20,16},{24,28},{28,24},{1,5},{5... | collective-permute-start | bytes 294920 | tf_op jit(solution)/shard_map/ppermute | solution.py:19
  61.3 10.6 %copy-start.7 = (bf16[4,160,128]{2,1,0:T(8,128)(2,1)}, bf16[4,160,128]{2,1,0:T(8,128)(2,1)S(1)}, u32[]{:S(2)}) copy-start(bf16[4,160,128]{2,1,0:T(8,128)(2,1)S(1)} %collective-permute-done.10.refs_9_) | copy-start | bytes 491524
  61.3 8.4 %collective-permute-start.5 = (bf16[4,96,128]{2,1,0:T(8,128)(2,1)}, bf16[4,96,128]{2,1,0:T(8,128)(2,1)S(1)}, u32[]{:S(2)}, u32[]{:S(2)}) collective-permute-start(bf16[4,96,128]{2,1,0:T(8,128)(2,1)} %get-tuple-element.19), channel_id=1, source_target_pairs={{0,8},{4,12},{8,0},{12,4},{16,24},{20,28},{24,16},{28,20},{1,9},{5... | collective-permute-start | bytes 294920 | tf_op jit(solution)/shard_map/ppermute | solution.py:19
  64.4 6.9 %collective-permute-start.6 = (bf16[4,96,128]{2,1,0:T(8,128)(2,1)}, bf16[4,96,128]{2,1,0:T(8,128)(2,1)S(1)}, u32[]{:S(2)}, u32[]{:S(2)}) collective-permute-start(bf16[4,96,128]{2,1,0:T(8,128)(2,1)} %get-tuple-element.20), channel_id=1, source_target_pairs={{0,12},{4,8},{8,4},{12,0},{16,28},{20,24},{24,20},{28,16},{1,13},{... | collective-permute-start | bytes 294920 | tf_op jit(solution)/shard_map/ppermute | solution.py:19
  78.2 1.5 %collective-permute-start.11 = (f32[3,8,128]{2,1,0:T(8,128)}, f32[3,8,128]{2,1,0:T(8,128)S(1)}, u32[]{:S(2)}, u32[]{:S(2)}) collective-permute-start(f32[3,8,128]{2,1,0:T(8,128)} %get-tuple-element.26), channel_id=1, source_target_pairs={{0,1},{1,0},{2,3},{3,2},{4,5},{5,4},{6,7},{7,6},{8,9},{9,8},{10,11... | collective-permute-start | bytes 36872 | tf_op jit(solution)/shard_map/ppermute | solution.py:19
  80.3 3.7 %collective-permute-start.12 = (f32[3,8,128]{2,1,0:T(8,128)S(1)}, f32[3,8,128]{2,1,0:T(8,128)S(1)}, u32[]{:S(2)}, u32[]{:S(2)}) collective-permute-start(f32[3,8,128]{2,1,0:T(8,128)S(1)} %add.64), channel_id=1, source_target_pairs={{0,2},{1,3},{2,0},{3,1},{4,6},{5,7},{6,4},{7,5},{8,10},{9,11},{10,... | collective-permute-start | bytes 36872 | tf_op jit(solution)/shard_map/ppermute | solution.py:19
  84.0 3.7 %collective-permute-start.13 = (f32[3,8,128]{2,1,0:T(8,128)S(1)}, f32[3,8,128]{2,1,0:T(8,128)S(1)}, u32[]{:S(2)}, u32[]{:S(2)}) collective-permute-start(f32[3,8,128]{2,1,0:T(8,128)S(1)} %add.65), channel_id=1, source_target_pairs={{0,4},{4,0},{8,12},{12,8},{16,20},{20,16},{24,28},{28,24},{1,5},{5... | collective-permute-start | bytes 36872 | tf_op jit(solution)/shard_map/ppermute | solution.py:19
  87.7 3.7 %collective-permute-start.14 = (f32[3,8,128]{2,1,0:T(8,128)S(1)}, f32[3,8,128]{2,1,0:T(8,128)S(1)}, u32[]{:S(2)}, u32[]{:S(2)}) collective-permute-start(f32[3,8,128]{2,1,0:T(8,128)S(1)} %add.66), channel_id=1, source_target_pairs={{0,8},{4,12},{8,0},{12,4},{16,24},{20,28},{24,16},{28,20},{1,9},{5... | collective-permute-start | bytes 36872 | tf_op jit(solution)/shard_map/ppermute | solution.py:19
  91.4 4.6 %collective-permute-start.15 = (f32[3,8,128]{2,1,0:T(8,128)S(1)}, f32[3,8,128]{2,1,0:T(8,128)S(1)}, u32[]{:S(2)}, u32[]{:S(2)}) collective-permute-start(f32[3,8,128]{2,1,0:T(8,128)S(1)} %add.67), channel_id=1, source_target_pairs={{0,16},{4,20},{8,24},{12,28},{16,0},{20,4},{24,8},{28,12},{1,17},{... | collective-permute-start | bytes 36872 | tf_op jit(solution)/shard_map/ppermute | solution.py:19
  (7 other events, 26.1 us)
where the time goes:
time: 97.3 us; the launch traced here: 96.6 us
  waiting for transfers between devices  40.6 us (42%)
  starting transfers between devices  30.7 us (32%)
  Pallas kernels  14.2 us (15%)
  other arithmetic  5.17 us (5%)
  local copies, waits for them, and re-layouts  5.06 us (5%)
    ppermute x16, waiting for transfers between devices, swap(): return lax.ppermute(x, axis, [(i, i ^ bits) for i in range(size)])  39 us
    ppermute x16, starting transfers between devices, swap(): return lax.ppermute(x, axis, [(i, i ^ bits) for i in range(size)])  23.4 us
    pallas_call x3, Pallas kernels, gather_rows(): pl.pallas_call(body, in_specs=[SMEM, ANY], out_specs=[pl.BlockSpec(memory...  8 us
    all_to_all x1, starting transfers between devices, body(): lax.all_to_all(request, 'tm', split_axis=0, concat_axis=0, tiled=True)  7.31 us
    pallas_call x1, Pallas kernels, departures_kernel(): pl.pallas_call(body, grid=(groups // STEP,), in_specs=[SMEM] * 4 + [pl.Bl...  6.17 us
  transfers between devices with their start and end apart: 17, of which 11 were waited for; matrix products, arithmetic and copies ran while one was open for 5% of the time, Pallas kernels for 8%

commit v1 on v0

--- a/solution.py
+++ b/solution.py
@@ -19,35 +19,84 @@
     return lax.ppermute(x, axis, [(i, i ^ bits) for i in range(size)])
 
 
-def gather_rows(ids, slab, pieces, first, rows):
+def index_kernel(win_of, block, me, windows):
+    groups = win_of.shape[0]
+    opposite = windows - 2
+
+    def body(win_ref, block_ref, me_ref, request_ref, slot_ref, count_ref):
+        def clear(w, carry):
+            count_ref[w] = 0
+            for k in range(2 * GCAP):
+                request_ref[w, k] = 0
+            return carry
+
+        lax.fori_loop(0, windows, clear, 0)
+        mine = me_ref[0]
+
+        def place(g, carry):
+            w = win_ref[g]
+            rank = count_ref[w]
+            count_ref[w] = rank + 1
+            request_ref[w, rank] = block_ref[g]
+            request_ref[w ^ opposite, GCAP + rank] = block_ref[g]
+            slot_ref[g] = (w ^ mine) * GCAP + rank
+            return carry
+
+        lax.fori_loop(0, groups, place, 0)
+
+    return pl.pallas_call(
+        body,
+        in_specs=[SMEM] * 3,
+        out_specs=[SMEM] * 2,
+        out_shape=[
+            jax.ShapeDtypeStruct((windows, 2 * GCAP), jnp.int32),
+            jax.ShapeDtypeStruct((groups,), jnp.int32),
+        ],
+        scratch_shapes=[pltpu.SMEM((windows,), jnp.int32)],
+    )(win_of, block, me)
+
+
+def gather_rows(asked, me, slab, partners, column, first, rows):
     width = slab.shape[2]
-
-    def body(ids_ref, slab_ref, *refs):
-        outs, sems = refs[:pieces], refs[pieces]
-        copies = []
+    pieces = len(partners)
+
+    def body(asked_ref, me_ref, slab_ref, *refs):
+        outs, stages, arrived, left = refs[:pieces], *refs[pieces:]
+        loads, stores = [], []
+        for piece, j in enumerate(partners):
+            source = j ^ me_ref[0]
+            for k in range(GCAP):
+                copy = pltpu.make_async_copy(
+                    slab_ref.at[asked_ref[source, column + k], pl.ds(first, rows)],
+                    stages.at[piece, k],
+                    arrived.at[piece * GCAP + k],
+                )
+                copy.start()
+                loads.append(copy)
         for piece in range(pieces):
             for k in range(GCAP):
-                copy = pltpu.make_async_copy(
-                    slab_ref.at[ids_ref[piece, k], pl.ds(first, rows)],
-                    outs[piece].at[k],
-                    sems.at[piece * GCAP + k],
-                )
-                copy.start()
-                copies.append(copy)
-        for copy in copies:
+                loads[piece * GCAP + k].wait()
+            copy = pltpu.make_async_copy(stages.at[piece], outs[piece], left.at[piece])
+            copy.start()
+            stores.append(copy)
+        for copy in stores:
             copy.wait()
 
     return pl.pallas_call(
         body,
-        in_specs=[SMEM, ANY],
-        out_specs=[pl.BlockSpec(memory_space=pltpu.VMEM)] * pieces,
+        in_specs=[SMEM, SMEM, ANY],
+        out_specs=[ANY] * pieces,
         out_shape=[jax.ShapeDtypeStruct((GCAP, rows, width), slab.dtype)] * pieces,
-        scratch_shapes=[pltpu.SemaphoreType.DMA((pieces * GCAP,))],
-    )(ids, slab)
+        scratch_shapes=[
+            pltpu.VMEM((pieces, GCAP, rows, width), slab.dtype),
+            pltpu.SemaphoreType.DMA((pieces * GCAP,)),
+            pltpu.SemaphoreType.DMA((pieces,)),
+        ],
+    )(asked, me, slab)
 
 
 def departures_kernel(
-    slab, mirror, near, far_low, far_high, slot_of, win_of, own_ids, mirror_ids, weights, observed, used_t, inv_error,
+    slab, mirror, near, far_low, far_high, slot_of, win_of, request, me, weights, observed, used_t, inv_error,
     kept_rows, low,
 ):
     groups, slots, cells = weights.shape
@@ -58,7 +107,7 @@
     opposite = windows - 2
     n_sems = 2 * GCAP + n_near + n_low + n_high
 
-    def body(slot_ref, win_ref, own_ref, mir_ref, w_ref, y_ref, u_ref, inv_ref, kept_ref, slab_ref, mirror_ref, *refs):
+    def body(slot_ref, win_ref, request_ref, me_ref, w_ref, y_ref, u_ref, inv_ref, kept_ref, slab_ref, mirror_ref, *refs):
         near_refs = refs[:n_near]
         low_refs = refs[n_near:n_near + n_low]
         high_refs = refs[n_near + n_low:n_near + n_low + n_high]
@@ -75,8 +124,8 @@
                 copies.append(copy)
 
             for k in range(GCAP):
-                add(slab_ref.at[own_ref[k]], x_ref.at[k])
-                add(mirror_ref.at[mir_ref[k]], x_ref.at[opposite * GCAP + k, pl.ds(0, low)])
+                add(slab_ref.at[request_ref[me_ref[0], k]], x_ref.at[k])
+                add(mirror_ref.at[request_ref[me_ref[0], GCAP + k]], x_ref.at[opposite * GCAP + k, pl.ds(0, low)])
             for j in range(1, half):
                 add(near_refs[j - 1], x_ref.at[pl.ds(j * GCAP, GCAP)])
                 add(low_refs[j - 1], x_ref.at[pl.ds((j ^ opposite) * GCAP, GCAP), pl.ds(0, low)])
@@ -124,7 +173,7 @@
             pltpu.SemaphoreType.DMA((n_sems,)),
         ],
     )(
-        slot_of, win_of, own_ids, mirror_ids, weights, observed, used_t, inv_error[None, :], kept_rows,
+        slot_of, win_of, request, me, weights, observed, used_t, inv_error[None, :], kept_rows,
         slab, mirror, *near, *far_low, *far_high,
     )
 
@@ -135,30 +184,24 @@
     windows = lax.axis_size("tm")
     half = windows // 2
     opposite = windows - 2
-    low = cells * 3 // 8 // 16 * 16
-    me = lax.axis_index("tm")
+    low = cells * 5 // 8 // 16 * 16
+    me = lax.axis_index("tm").reshape(1)
     slab = trajectory[0]
 
     mirror = swap(slab[:, :low], "tm", opposite)
 
     win_of = window[:, 0]
-    gid = jnp.arange(groups, dtype=jnp.int32)
-    rank = jnp.sum(((win_of[:, None] == win_of[None, :]) & (gid[None, :] < gid[:, None])).astype(jnp.int32), 1)
-    code = win_of * GCAP + rank
-    wanted = jnp.sum(
-        jnp.where(code[None, :] == jnp.arange(windows * GCAP, dtype=jnp.int32)[:, None], block[None, :], 0), 1
-    ).reshape(windows, GCAP)
-    across = wanted.reshape(2, half // 2, 2, GCAP)[::-1, ::-1].reshape(windows, GCAP)
-    request = jnp.concatenate([wanted, across], 1)
-    asked = lax.all_to_all(request, "tm", split_axis=0, concat_axis=0, tiled=True)
-    by_xor = asked[jnp.arange(windows, dtype=jnp.int32) ^ me]
-
-    send_high = gather_rows(by_xor[half:, :GCAP], slab, half, low, cells - low)
-    far_high = [swap(send_high[j - half], "tm", j) for j in range(half, windows)]
-    send_near = gather_rows(by_xor[1:half, :GCAP], slab, half - 1, 0, cells)
-    near = [swap(send_near[j - 1], "tm", j) for j in range(1, half)]
-    send_low = gather_rows(by_xor[1:half, GCAP:], mirror, half - 1, 0, low)
-    far_low = [swap(send_low[j - 1], "tm", j) for j in range(1, half)]
+    request, slot_of = index_kernel(win_of, block, me, windows)
+    asked = lax.all_to_all(request[:, None], "tm", split_axis=0, concat_axis=0, tiled=True)[:, 0]
+
+    far = tuple(range(half, windows))
+    close = tuple(range(1, half))
+    sent = gather_rows(asked, me, slab, far, 0, low, cells - low)
+    far_high = [swap(part, "tm", j) for j, part in zip(far, sent)]
+    sent = gather_rows(asked, me, slab, close, 0, 0, cells)
+    near = [swap(part, "tm", j) for j, part in zip(close, sent)]
+    sent = gather_rows(asked, me, mirror, close, GCAP, 0, low)
+    far_low = [swap(part, "tm", j) for j, part in zip(close, sent)]
 
     slot_ids = lax.broadcasted_iota(jnp.int32, (groups, slots), 1)
     used = jnp.where(slot_ids < counts[:, None], flags, 0).astype(jnp.float32)
@@ -167,9 +210,8 @@
     kept = jnp.sum(jnp.where(member, jnp.sum(used, 1)[None, :], 0.0), 1)
     kept_rows = jnp.broadcast_to(kept[:, None], (windows, levels))
 
-    slot_of = (win_of ^ me) * GCAP + rank
     departures, sums = departures_kernel(
-        slab, mirror, near, far_low, far_high, slot_of, win_of, wanted[me], wanted[me ^ opposite], weights, observed,
+        slab, mirror, near, far_low, far_high, slot_of, win_of, request, me, weights, observed,
         used_t, inv_error, kept_rows, low,
     )
     for axis in ("obs", "tm"):
@@ -177,7 +219,7 @@
         while bits < lax.axis_size(axis):
             sums = sums + swap(sums, axis, bits)
             bits *= 2
-    mine = lax.dynamic_slice_in_dim(sums, me, 1, 1)
+    mine = lax.dynamic_slice_in_dim(sums, me[0], 1, 1)
     window_bias = mine[0] / jnp.sqrt(mine[2] + 1.0)
     window_chi = mine[1] / (mine[2] + 1.0)
     return (departures, window_bias, window_chi)

time: 97.3 us -> 99.7 us (1.025)
  blocking collectives: 0 us -> 27.2 us
  waiting for transfers between devices: 40.6 us -> 28.1 us
  starting transfers between devices: 30.7 us -> 22.8 us
  other arithmetic: 5.17 us -> 1.62 us
  local copies, waits for them, and re-layouts: 5.06 us -> 2.71 us
  Pallas kernels: 14.2 us -> 15.7 us
    all_to_all x0 -> x1, blocking collectives: none -> 27.2 us  [body(): lax.all_to_all(request[:, None], 'tm', split_axis=0, concat_axis=0, tiled...]
    ppermute x16, waiting for transfers between devices: 39 us -> 28.1 us  [swap(): return lax.ppermute(x, axis, [(i, i ^ bits) for i in range(size)])]
    all_to_all x1 -> x0, starting transfers between devices: 7.31 us -> none  [body(): lax.all_to_all(request, 'tm', split_axis=0, concat_axis=0, tiled=True)]
    reduce_sum x2 -> x0, other arithmetic: 1.67 us -> none  [the longest x1 0.91 us: body(): jnp.sum(((win_of[:, None] == win_of[None, :]) & (gid[None, :] < gid[:, No...]
    all_to_all x1 -> x0, waiting for transfers between devices: 1.6 us -> none  [body(): lax.all_to_all(request, 'tm', split_axis=0, concat_axis=0, tiled=True)]
    pallas_call x3 -> x4, Pallas kernels: 8 us -> 9.55 us  [the longest x3 7.73 us: gather_rows(): pl.pallas_call(body, in_specs=[SMEM, SMEM, ANY], out_specs=[ANY] * pieces...]
    slice x2 -> x0, local copies, waits for them, and re-layouts: 1.25 us -> none  [the longest x1 0.66 us: body(): send_low = gather_rows(by_xor[1:half, GCAP:], mirror, half - 1, 0, low)]
    add x1 -> x0, other arithmetic: 1.18 us -> none  [body(): code = win_of * GCAP + rank]
  transfers between devices with their start and end apart: 17 -> 16, of which waited for: 11 -> 9; matrix products, arithmetic and copies ran while one was open for 5% -> 1% of each run, Pallas kernels for 8% -> 10%
where the time goes in v1:
time: 99.7 us; the launch traced here: 99 us
  waiting for transfers between devices  28.1 us (28%)
  blocking collectives  27.2 us (27%)
  starting transfers between devices  22.8 us (23%)
  Pallas kernels  15.7 us (16%)
  local copies, waits for them, and re-layouts  2.71 us (3%)
  other arithmetic  1.62 us (2%)
    ppermute x16, waiting for transfers between devices, swap(): return lax.ppermute(x, axis, [(i, i ^ bits) for i in range(size)])  28.1 us
    all_to_all x1, blocking collectives, body(): lax.all_to_all(request[:, None], 'tm', split_axis=0, concat_axis=0, tiled...  27.2 us
    ppermute x16, starting transfers between devices, swap(): return lax.ppermute(x, axis, [(i, i ^ bits) for i in range(size)])  22.8 us
    pallas_call x3, Pallas kernels, gather_rows(): pl.pallas_call(body, in_specs=[SMEM, SMEM, ANY], out_specs=[ANY] * pieces...  7.73 us
    pallas_call x1, Pallas kernels, departures_kernel(): pl.pallas_call(body, grid=(groups // STEP,), in_specs=[SMEM] * 4 + [pl.Bl...  6.14 us
  transfers between devices with their start and end apart: 16, of which 9 were waited for; matrix products, arithmetic and copies ran while one was open for 1% of the time, Pallas kernels for 10%

profile of v1, /device:TPU:0, one launch (start us, length us, event | category | flops | bytes accessed | tf_op | source)
XLA Modules:
  0.0 99.0 jit_solution(12461705063426485345)
XLA Ops:
  0.7 1.1 %slice.17 = bf16[16,160,128]{2,1,0:T(8,128)(2,1)S(1)} slice(bf16[16,256,128]{2,1,0:T(8,128)(2,1)} %bitcast.15), slice={[0:16], [0:160], [0:128]} | slice | bytes 1310720 | tf_op jit(solution)/shard_map/slice | solution.py:191
  1.8 5.1 %collective-permute-start = (bf16[16,160,128]{2,1,0:T(8,128)(2,1)S(1)}, bf16[16,160,128]{2,1,0:T(8,128)(2,1)S(1)}, u32[]{:S(2)}, u32[]{:S(2)}) collective-permute-start(bf16[16,160,128]{2,1,0:T(8,128)(2,1)S(1)} %slice.17), channel_id=1, source_target_pairs={{0,24},{4,28},{8,16},{12,20},{16,8},{20,12},{24,0},{28,4},{1,25},{... | collective-permute-start | bytes 1966088 | tf_op jit(solution)/shard_map/ppermute | solution.py:19
  7.0 1.8 %shard_map.103 = (s32[8,8]{1,0:T(8,128)}, s32[32]{0:T(128)}) custom-call(s32[32]{0:T(128)} %bitcast.24, s32[32]{0:T(128)} %block_ref.1, s32[1]{0:T(128)} %bitcast.1.me_ref), custom_call_target="tpu_custom_call" | custom-call | tf_op jit(solution)/shard_map/pallas_call | solution.py:47
  8.8 27.2 %all_to_all.5 = s32[8,1,8]{2,1,0:T(1,128)} all-to-all(s32[8,1,8]{2,1,0:T(1,128)} %bitcast.23), channel_id=1, replica_groups=mesh['tm'=8,'obs'=4] {'tm'}, dimensions={0} | all-to-all | bytes 512 | tf_op jit(solution)/shard_map/all_to_all | solution.py:195
  36.0 2.5 %shard_map.106 = (bf16[4,96,128]{2,1,0:T(8,128)(2,1)}, bf16[4,96,128]{2,1,0:T(8,128)(2,1)}, bf16[4,96,128]{2,1,0:T(8,128)(2,1)}, bf16[4,96,128]{2,1,0:T(8,128)(2,1)}) custom-call(s32[8,8]{1,0:T(8,128)} %bitcast.20, s32[1]{0:T(128)} %bitcast.1.me_ref, bf16[16,256,128]{2,1,0:T(8,128)(2,1)} %bitcast.16), custom_call_target="tpu_custom_call" | custom-call | tf_op jit(solution)/shard_map/pallas_call | solution.py:85
  38.5 2.6 %collective-permute-start.10 = (bf16[4,96,128]{2,1,0:T(8,128)(2,1)}, bf16[4,96,128]{2,1,0:T(8,128)(2,1)S(1)}, u32[]{:S(2)}, u32[]{:S(2)}) collective-permute-start(bf16[4,96,128]{2,1,0:T(8,128)(2,1)} %get-tuple-element.28), channel_id=1, source_target_pairs={{0,28},{4,24},{8,20},{12,16},{16,12},{20,8},{24,4},{28,0},{1,29},{... | collective-permute-start | bytes 294920 | tf_op jit(solution)/shard_map/ppermute | solution.py:19
  41.1 2.7 %shard_map.104 = (bf16[4,256,128]{2,1,0:T(8,128)(2,1)}, bf16[4,256,128]{2,1,0:T(8,128)(2,1)}, bf16[4,256,128]{2,1,0:T(8,128)(2,1)}) custom-call(s32[8,8]{1,0:T(8,128)} %bitcast.21, s32[1]{0:T(128)} %bitcast.1.me_ref, bf16[16,256,128]{2,1,0:T(8,128)(2,1)} %bitcast.17), custom_call_target="tpu_custom_call" | custom-call | tf_op jit(solution)/shard_map/pallas_call | solution.py:85
  43.9 1.5 %collective-permute-start.1 = (bf16[4,256,128]{2,1,0:T(8,128)(2,1)}, bf16[4,256,128]{2,1,0:T(8,128)(2,1)S(1)}, u32[]{:S(2)}, u32[]{:S(2)}) collective-permute-start(bf16[4,256,128]{2,1,0:T(8,128)(2,1)} %get-tuple-element.19), channel_id=1, source_target_pairs={{0,4},{4,0},{8,12},{12,8},{16,20},{20,16},{24,28},{28,24},{1,5},{5... | collective-permute-start | bytes 786440 | tf_op jit(solution)/shard_map/ppermute | solution.py:19
  45.4 2.9 %collective-permute-start.8 = (bf16[4,96,128]{2,1,0:T(8,128)(2,1)}, bf16[4,96,128]{2,1,0:T(8,128)(2,1)S(1)}, u32[]{:S(2)}, u32[]{:S(2)}) collective-permute-start(bf16[4,96,128]{2,1,0:T(8,128)(2,1)} %get-tuple-element.26), channel_id=1, source_target_pairs={{0,20},{4,16},{8,28},{12,24},{16,4},{20,0},{24,12},{28,8},{1,21},{... | collective-permute-start | bytes 294920 | tf_op jit(solution)/shard_map/ppermute | solution.py:19
  48.3 1.3 %collective-permute-start.9 = (bf16[4,96,128]{2,1,0:T(8,128)(2,1)}, bf16[4,96,128]{2,1,0:T(8,128)(2,1)S(1)}, u32[]{:S(2)}, u32[]{:S(2)}) collective-permute-start(bf16[4,96,128]{2,1,0:T(8,128)(2,1)} %get-tuple-element.27), channel_id=1, source_target_pairs={{0,24},{4,28},{8,16},{12,20},{16,8},{20,12},{24,0},{28,4},{1,25},{... | collective-permute-start | bytes 294920 | tf_op jit(solution)/shard_map/ppermute | solution.py:19
  49.6 4.2 %collective-permute-done.7.refs_6_ = bf16[4,96,128]{2,1,0:T(8,128)(2,1)S(1)} collective-permute-done((bf16[4,96,128]{2,1,0:T(8,128)(2,1)}, bf16[4,96,128]{2,1,0:T(8,128)(2,1)S(1)}, u32[]{:S(2)}, u32[]{:S(2)}) %collective-permute-start.7) | collective-permute-done | bytes 98336 | tf_op jit(solution)/shard_map/ppermute | solution.py:19
  53.8 2.6 %collective-permute-start.3 = (bf16[4,256,128]{2,1,0:T(8,128)(2,1)}, bf16[4,256,128]{2,1,0:T(8,128)(2,1)S(1)}, u32[]{:S(2)}, u32[]{:S(2)}) collective-permute-start(bf16[4,256,128]{2,1,0:T(8,128)(2,1)} %get-tuple-element.21), channel_id=1, source_target_pairs={{0,12},{4,8},{8,4},{12,0},{16,28},{20,24},{24,20},{28,16},{1,13},{... | collective-permute-start | bytes 786440 | tf_op jit(solution)/shard_map/ppermute | solution.py:19
  56.5 2.5 %shard_map.105 = (bf16[4,160,128]{2,1,0:T(8,128)(2,1)}, bf16[4,160,128]{2,1,0:T(8,128)(2,1)}, bf16[4,160,128]{2,1,0:T(8,128)(2,1)}) custom-call(s32[8,8]{1,0:T(8,128)} %bitcast.22, s32[1]{0:T(128)} %bitcast.1.me_ref, bf16[16,160,128]{2,1,0:T(8,128)(2,1)} %copy-done), custom_call_target="tpu_custom_call" | custom-call | tf_op jit(solution)/shard_map/pallas_call | solution.py:85
  60.5 2.1 %collective-permute-start.6 = (bf16[4,160,128]{2,1,0:T(8,128)(2,1)}, bf16[4,160,128]{2,1,0:T(8,128)(2,1)S(1)}, u32[]{:S(2)}, u32[]{:S(2)}) collective-permute-start(bf16[4,160,128]{2,1,0:T(8,128)(2,1)} %get-tuple-element.24), channel_id=1, source_target_pairs={{0,12},{4,8},{8,4},{12,0},{16,28},{20,24},{24,20},{28,16},{1,13},{... | collective-permute-start | bytes 491528 | tf_op jit(solution)/shard_map/ppermute | solution.py:19
  63.8 5.6 %collective-permute-done.3.refs_2_ = bf16[4,256,128]{2,1,0:T(8,128)(2,1)S(1)} collective-permute-done((bf16[4,256,128]{2,1,0:T(8,128)(2,1)}, bf16[4,256,128]{2,1,0:T(8,128)(2,1)S(1)}, u32[]{:S(2)}, u32[]{:S(2)}) %collective-permute-start.3) | collective-permute-done | bytes 262176 | tf_op jit(solution)/shard_map/ppermute | solution.py:19
  69.4 1.9 %collective-permute-done.5.refs_4_ = bf16[4,160,128]{2,1,0:T(8,128)(2,1)S(1)} collective-permute-done((bf16[4,160,128]{2,1,0:T(8,128)(2,1)}, bf16[4,160,128]{2,1,0:T(8,128)(2,1)S(1)}, u32[]{:S(2)}, u32[]{:S(2)}) %collective-permute-start.5) | collective-permute-done | bytes 163872 | tf_op jit(solution)/shard_map/ppermute | solution.py:19
  71.3 2.4 %collective-permute-done.6.refs_5_ = bf16[4,160,128]{2,1,0:T(8,128)(2,1)S(1)} collective-permute-done((bf16[4,160,128]{2,1,0:T(8,128)(2,1)}, bf16[4,160,128]{2,1,0:T(8,128)(2,1)S(1)}, u32[]{:S(2)}, u32[]{:S(2)}) %collective-permute-start.6) | collective-permute-done | bytes 163872 | tf_op jit(solution)/shard_map/ppermute | solution.py:19
  74.5 6.1 %shard_map.107 = (bf16[32,128,128]{2,1,0:T(8,128)(2,1)}, f32[3,8,128]{2,1,0:T(8,128)}) custom-call(s32[32]{0:T(128)} %get-tuple-element.17.slot_ref, s32[32]{0:T(128)} %bitcast.25, s32[8,8]{1,0:T(8,128)} %get-tuple-element.18.request_ref, s32[1]{0:T(128)} %bitcast.1.me_ref, bf16[32,128,256]{2,1,0:T(8,128)(2,1)} %w_ref.1, bf16[32,128,128]{2,1,0:T(8,128)(2,1)} %y_ref.1, ...), custom_call_target="tpu_custom_call" | custom-call | tf_op jit(solution)/shard_map/pallas_call | solution.py:151
  80.7 1.4 %collective-permute-done.11 = f32[3,8,128]{2,1,0:T(8,128)S(1)} collective-permute-done((f32[3,8,128]{2,1,0:T(8,128)}, f32[3,8,128]{2,1,0:T(8,128)S(1)}, u32[]{:S(2)}, u32[]{:S(2)}) %collective-permute-start.11) | collective-permute-done | bytes 12320 | tf_op jit(solution)/shard_map/ppermute | solution.py:19
  82.8 1.5 %collective-permute-start.12 = (f32[3,8,128]{2,1,0:T(8,128)S(1)}, f32[3,8,128]{2,1,0:T(8,128)S(1)}, u32[]{:S(2)}, u32[]{:S(2)}) collective-permute-start(f32[3,8,128]{2,1,0:T(8,128)S(1)} %add.35), channel_id=1, source_target_pairs={{0,2},{1,3},{2,0},{3,1},{4,6},{5,7},{6,4},{7,5},{8,10},{9,11},{10,... | collective-permute-start | bytes 36872 | tf_op jit(solution)/shard_map/ppermute | solution.py:19
  84.3 2.2 %collective-permute-done.12 = f32[3,8,128]{2,1,0:T(8,128)S(1)} collective-permute-done((f32[3,8,128]{2,1,0:T(8,128)S(1)}, f32[3,8,128]{2,1,0:T(8,128)S(1)}, u32[]{:S(2)}, u32[]{:S(2)}) %collective-permute-start.12) | collective-permute-done | bytes 12320 | tf_op jit(solution)/shard_map/ppermute | solution.py:19
  87.3 2.9 %collective-permute-done.13 = f32[3,8,128]{2,1,0:T(8,128)S(1)} collective-permute-done((f32[3,8,128]{2,1,0:T(8,128)S(1)}, f32[3,8,128]{2,1,0:T(8,128)S(1)}, u32[]{:S(2)}, u32[]{:S(2)}) %collective-permute-start.13) | collective-permute-done | bytes 12320 | tf_op jit(solution)/shard_map/ppermute | solution.py:19
  90.2 3.7 %collective-permute-done.14 = f32[3,8,128]{2,1,0:T(8,128)S(1)} collective-permute-done((f32[3,8,128]{2,1,0:T(8,128)S(1)}, f32[3,8,128]{2,1,0:T(8,128)S(1)}, u32[]{:S(2)}, u32[]{:S(2)}) %collective-permute-start.14) | collective-permute-done | bytes 12320 | tf_op jit(solution)/shard_map/ppermute | solution.py:19
  94.7 3.8 %collective-permute-done.15 = f32[3,8,128]{2,1,0:T(8,128)S(1)} collective-permute-done((f32[3,8,128]{2,1,0:T(8,128)S(1)}, f32[3,8,128]{2,1,0:T(8,128)S(1)}, u32[]{:S(2)}, u32[]{:S(2)}) %collective-permute-start.15) | collective-permute-done | bytes 12320 | tf_op jit(solution)/shard_map/ppermute | solution.py:19
  (54 shorter events, 6.3 us)
Async XLA Ops:
  0.6 55.8 %copy-start.12 = (s32[32]{0:T(128)S(1)}, s32[32]{0:T(128)}, u32[]{:S(2)}) copy-start(s32[32]{0:T(128)} %param.13) | copy-start | bytes 388
  0.6 55.8 %copy-start.11 = (s32[32,128]{1,0:T(8,128)S(1)}, s32[32,128]{1,0:T(8,128)}, u32[]{:S(2)}) copy-start(s32[32,128]{1,0:T(8,128)} %param.14) | copy-start | bytes 49156
  0.7 63.0 %copy-start.13 = (s32[32,1]{0,1:T(1,128)S(1)}, s32[32,1]{0,1:T(1,128)}, u32[]{:S(2)}) copy-start(s32[32,1]{0,1:T(1,128)} %param.11) | copy-start | bytes 388
  1.8 52.0 %collective-permute-start = (bf16[16,160,128]{2,1,0:T(8,128)(2,1)S(1)}, bf16[16,160,128]{2,1,0:T(8,128)(2,1)S(1)}, u32[]{:S(2)}, u32[]{:S(2)}) collective-permute-start(bf16[16,160,128]{2,1,0:T(8,128)(2,1)S(1)} %slice.17), channel_id=1, source_target_pairs={{0,24},{4,28},{8,16},{12,20},{16,8},{20,12},{24,0},{28,4},{1,25},{... | collective-permute-start | bytes 1966088 | tf_op jit(solution)/shard_map/ppermute | solution.py:19
  38.5 9.8 %collective-permute-start.10 = (bf16[4,96,128]{2,1,0:T(8,128)(2,1)}, bf16[4,96,128]{2,1,0:T(8,128)(2,1)S(1)}, u32[]{:S(2)}, u32[]{:S(2)}) collective-permute-start(bf16[4,96,128]{2,1,0:T(8,128)(2,1)} %get-tuple-element.28), channel_id=1, source_target_pairs={{0,28},{4,24},{8,20},{12,16},{16,12},{20,8},{24,4},{28,0},{1,29},{... | collective-permute-start | bytes 294920 | tf_op jit(solution)/shard_map/ppermute | solution.py:19
  41.1 12.6 %collective-permute-start.7 = (bf16[4,96,128]{2,1,0:T(8,128)(2,1)}, bf16[4,96,128]{2,1,0:T(8,128)(2,1)S(1)}, u32[]{:S(2)}, u32[]{:S(2)}) collective-permute-start(bf16[4,96,128]{2,1,0:T(8,128)(2,1)} %get-tuple-element.25), channel_id=1, source_target_pairs={{0,16},{4,20},{8,24},{12,28},{16,0},{20,4},{24,8},{28,12},{1,17},{... | collective-permute-start | bytes 294920 | tf_op jit(solution)/shard_map/ppermute | solution.py:19
  43.9 16.7 %collective-permute-start.1 = (bf16[4,256,128]{2,1,0:T(8,128)(2,1)}, bf16[4,256,128]{2,1,0:T(8,128)(2,1)S(1)}, u32[]{:S(2)}, u32[]{:S(2)}) collective-permute-start(bf16[4,256,128]{2,1,0:T(8,128)(2,1)} %get-tuple-element.19), channel_id=1, source_target_pairs={{0,4},{4,0},{8,12},{12,8},{16,20},{20,16},{24,28},{28,24},{1,5},{5... | collective-permute-start | bytes 786440 | tf_op jit(solution)/shard_map/ppermute | solution.py:19
  45.4 13.6 %collective-permute-start.8 = (bf16[4,96,128]{2,1,0:T(8,128)(2,1)}, bf16[4,96,128]{2,1,0:T(8,128)(2,1)S(1)}, u32[]{:S(2)}, u32[]{:S(2)}) collective-permute-start(bf16[4,96,128]{2,1,0:T(8,128)(2,1)} %get-tuple-element.26), channel_id=1, source_target_pairs={{0,20},{4,16},{8,28},{12,24},{16,4},{20,0},{24,12},{28,8},{1,21},{... | collective-permute-start | bytes 294920 | tf_op jit(solution)/shard_map/ppermute | solution.py:19
  48.3 26.1 %copy-start.7 = (bf16[4,96,128]{2,1,0:T(8,128)(2,1)}, bf16[4,96,128]{2,1,0:T(8,128)(2,1)S(1)}, u32[]{:S(2)}) copy-start(bf16[4,96,128]{2,1,0:T(8,128)(2,1)S(1)} %collective-permute-done.10.refs_9_) | copy-start | bytes 294916
  48.3 11.7 %collective-permute-start.9 = (bf16[4,96,128]{2,1,0:T(8,128)(2,1)}, bf16[4,96,128]{2,1,0:T(8,128)(2,1)S(1)}, u32[]{:S(2)}, u32[]{:S(2)}) collective-permute-start(bf16[4,96,128]{2,1,0:T(8,128)(2,1)} %get-tuple-element.27), channel_id=1, source_target_pairs={{0,24},{4,28},{8,16},{12,20},{16,8},{20,12},{24,0},{28,4},{1,25},{... | collective-permute-start | bytes 294920 | tf_op jit(solution)/shard_map/ppermute | solution.py:19
  53.8 20.6 %copy-start.8 = (bf16[4,96,128]{2,1,0:T(8,128)(2,1)}, bf16[4,96,128]{2,1,0:T(8,128)(2,1)S(1)}, u32[]{:S(2)}) copy-start(bf16[4,96,128]{2,1,0:T(8,128)(2,1)S(1)} %collective-permute-done.7.refs_6_) | copy-start | bytes 294916
  53.8 10.0 %collective-permute-start.2 = (bf16[4,256,128]{2,1,0:T(8,128)(2,1)}, bf16[4,256,128]{2,1,0:T(8,128)(2,1)S(1)}, u32[]{:S(2)}, u32[]{:S(2)}) collective-permute-start(bf16[4,256,128]{2,1,0:T(8,128)(2,1)} %get-tuple-element.20), channel_id=1, source_target_pairs={{0,8},{4,12},{8,0},{12,4},{16,24},{20,28},{24,16},{28,20},{1,9},{5... | collective-permute-start | bytes 786440 | tf_op jit(solution)/shard_map/ppermute | solution.py:19
  53.8 15.6 %collective-permute-start.3 = (bf16[4,256,128]{2,1,0:T(8,128)(2,1)}, bf16[4,256,128]{2,1,0:T(8,128)(2,1)S(1)}, u32[]{:S(2)}, u32[]{:S(2)}) collective-permute-start(bf16[4,256,128]{2,1,0:T(8,128)(2,1)} %get-tuple-element.21), channel_id=1, source_target_pairs={{0,12},{4,8},{8,4},{12,0},{16,28},{20,24},{24,20},{28,16},{1,13},{... | collective-permute-start | bytes 786440 | tf_op jit(solution)/shard_map/ppermute | solution.py:19
  59.0 15.4 %copy-start.9 = (bf16[4,96,128]{2,1,0:T(8,128)(2,1)}, bf16[4,96,128]{2,1,0:T(8,128)(2,1)S(1)}, u32[]{:S(2)}) copy-start(bf16[4,96,128]{2,1,0:T(8,128)(2,1)S(1)} %collective-permute-done.8.refs_7_) | copy-start | bytes 294916
  59.0 10.4 %collective-permute-start.4 = (bf16[4,160,128]{2,1,0:T(8,128)(2,1)}, bf16[4,160,128]{2,1,0:T(8,128)(2,1)S(1)}, u32[]{:S(2)}, u32[]{:S(2)}) collective-permute-start(bf16[4,160,128]{2,1,0:T(8,128)(2,1)} %get-tuple-element.22), channel_id=1, source_target_pairs={{0,4},{4,0},{8,12},{12,8},{16,20},{20,16},{24,28},{28,24},{1,5},{5... | collective-permute-start | bytes 491528 | tf_op jit(solution)/shard_map/ppermute | solution.py:19
  60.0 14.5 %copy-start.10 = (bf16[4,96,128]{2,1,0:T(8,128)(2,1)}, bf16[4,96,128]{2,1,0:T(8,128)(2,1)S(1)}, u32[]{:S(2)}) copy-start(bf16[4,96,128]{2,1,0:T(8,128)(2,1)S(1)} %collective-permute-done.9.refs_8_) | copy-start | bytes 294916
  60.0 11.3 %collective-permute-start.5 = (bf16[4,160,128]{2,1,0:T(8,128)(2,1)}, bf16[4,160,128]{2,1,0:T(8,128)(2,1)S(1)}, u32[]{:S(2)}, u32[]{:S(2)}) collective-permute-start(bf16[4,160,128]{2,1,0:T(8,128)(2,1)} %get-tuple-element.23), channel_id=1, source_target_pairs={{0,8},{4,12},{8,0},{12,4},{16,24},{20,28},{24,16},{28,20},{1,9},{5... | collective-permute-start | bytes 491528 | tf_op jit(solution)/shard_map/ppermute | solution.py:19
  60.5 13.9 %copy-start.1 = (bf16[4,256,128]{2,1,0:T(8,128)(2,1)}, bf16[4,256,128]{2,1,0:T(8,128)(2,1)S(1)}, u32[]{:S(2)}) copy-start(bf16[4,256,128]{2,1,0:T(8,128)(2,1)S(1)} %collective-permute-done.1.refs_0_) | copy-start | bytes 786436
  60.5 13.2 %collective-permute-start.6 = (bf16[4,160,128]{2,1,0:T(8,128)(2,1)}, bf16[4,160,128]{2,1,0:T(8,128)(2,1)S(1)}, u32[]{:S(2)}, u32[]{:S(2)}) collective-permute-start(bf16[4,160,128]{2,1,0:T(8,128)(2,1)} %get-tuple-element.24), channel_id=1, source_target_pairs={{0,12},{4,8},{8,4},{12,0},{16,28},{20,24},{24,20},{28,16},{1,13},{... | collective-permute-start | bytes 491528 | tf_op jit(solution)/shard_map/ppermute | solution.py:19
  80.6 1.5 %collective-permute-start.11 = (f32[3,8,128]{2,1,0:T(8,128)}, f32[3,8,128]{2,1,0:T(8,128)S(1)}, u32[]{:S(2)}, u32[]{:S(2)}) collective-permute-start(f32[3,8,128]{2,1,0:T(8,128)} %get-tuple-element.30), channel_id=1, source_target_pairs={{0,1},{1,0},{2,3},{3,2},{4,5},{5,4},{6,7},{7,6},{8,9},{9,8},{10,11... | collective-permute-start | bytes 36872 | tf_op jit(solution)/shard_map/ppermute | solution.py:19
  82.8 3.7 %collective-permute-start.12 = (f32[3,8,128]{2,1,0:T(8,128)S(1)}, f32[3,8,128]{2,1,0:T(8,128)S(1)}, u32[]{:S(2)}, u32[]{:S(2)}) collective-permute-start(f32[3,8,128]{2,1,0:T(8,128)S(1)} %add.35), channel_id=1, source_target_pairs={{0,2},{1,3},{2,0},{3,1},{4,6},{5,7},{6,4},{7,5},{8,10},{9,11},{10,... | collective-permute-start | bytes 36872 | tf_op jit(solution)/shard_map/ppermute | solution.py:19
  86.5 3.7 %collective-permute-start.13 = (f32[3,8,128]{2,1,0:T(8,128)S(1)}, f32[3,8,128]{2,1,0:T(8,128)S(1)}, u32[]{:S(2)}, u32[]{:S(2)}) collective-permute-start(f32[3,8,128]{2,1,0:T(8,128)S(1)} %add.36), channel_id=1, source_target_pairs={{0,4},{4,0},{8,12},{12,8},{16,20},{20,16},{24,28},{28,24},{1,5},{5... | collective-permute-start | bytes 36872 | tf_op jit(solution)/shard_map/ppermute | solution.py:19
  90.2 3.7 %collective-permute-start.14 = (f32[3,8,128]{2,1,0:T(8,128)S(1)}, f32[3,8,128]{2,1,0:T(8,128)S(1)}, u32[]{:S(2)}, u32[]{:S(2)}) collective-permute-start(f32[3,8,128]{2,1,0:T(8,128)S(1)} %add.37), channel_id=1, source_target_pairs={{0,8},{4,12},{8,0},{12,4},{16,24},{20,28},{24,16},{28,20},{1,9},{5... | collective-permute-start | bytes 36872 | tf_op jit(solution)/shard_map/ppermute | solution.py:19
  93.9 4.6 %collective-permute-start.15 = (f32[3,8,128]{2,1,0:T(8,128)S(1)}, f32[3,8,128]{2,1,0:T(8,128)S(1)}, u32[]{:S(2)}, u32[]{:S(2)}) collective-permute-start(f32[3,8,128]{2,1,0:T(8,128)S(1)} %add.38), channel_id=1, source_target_pairs={{0,16},{4,20},{8,24},{12,28},{16,0},{20,4},{24,8},{28,12},{1,17},{... | collective-permute-start | bytes 36872 | tf_op jit(solution)/shard_map/ppermute | solution.py:19
  (6 other events, 27.4 us)

commit v2 on v1

--- a/solution.py
+++ b/solution.py
@@ -56,26 +56,34 @@
     )(win_of, block, me)
 
 
-def gather_rows(asked, me, slab, partners, column, first, rows):
-    width = slab.shape[2]
+def gather_rows(asked, me, sources, partners):
+    count = len(sources)
+    width = sources[0][0].shape[2]
+    dtype = sources[0][0].dtype
     pieces = len(partners)
-
-    def body(asked_ref, me_ref, slab_ref, *refs):
-        outs, stages, arrived, left = refs[:pieces], *refs[pieces:]
+    total = sum(rows for _, _, _, rows in sources)
+
+    def body(asked_ref, me_ref, *refs):
+        source_refs, outs = refs[:count], refs[count:count + pieces]
+        stages, arrived, left = refs[count + pieces:]
         loads, stores = [], []
         for piece, j in enumerate(partners):
-            source = j ^ me_ref[0]
+            asker = j ^ me_ref[0]
             for k in range(GCAP):
-                copy = pltpu.make_async_copy(
-                    slab_ref.at[asked_ref[source, column + k], pl.ds(first, rows)],
-                    stages.at[piece, k],
-                    arrived.at[piece * GCAP + k],
-                )
-                copy.start()
-                loads.append(copy)
+                at = 0
+                for ref, (_, column, first, rows) in zip(source_refs, sources):
+                    copy = pltpu.make_async_copy(
+                        ref.at[asked_ref[asker, column + k], pl.ds(first, rows)],
+                        stages.at[piece, k, pl.ds(at, rows)],
+                        arrived.at[len(loads)],
+                    )
+                    copy.start()
+                    loads.append(copy)
+                    at += rows
+        each = GCAP * count
         for piece in range(pieces):
-            for k in range(GCAP):
-                loads[piece * GCAP + k].wait()
+            for copy in loads[piece * each:(piece + 1) * each]:
+                copy.wait()
             copy = pltpu.make_async_copy(stages.at[piece], outs[piece], left.at[piece])
             copy.start()
             stores.append(copy)
@@ -84,34 +92,33 @@
 
     return pl.pallas_call(
         body,
-        in_specs=[SMEM, SMEM, ANY],
+        in_specs=[SMEM, SMEM] + [ANY] * count,
         out_specs=[ANY] * pieces,
-        out_shape=[jax.ShapeDtypeStruct((GCAP, rows, width), slab.dtype)] * pieces,
+        out_shape=[jax.ShapeDtypeStruct((GCAP, total, width), dtype)] * pieces,
         scratch_shapes=[
-            pltpu.VMEM((pieces, GCAP, rows, width), slab.dtype),
-            pltpu.SemaphoreType.DMA((pieces * GCAP,)),
+            pltpu.VMEM((pieces, GCAP, total, width), dtype),
+            pltpu.SemaphoreType.DMA((pieces * GCAP * count,)),
             pltpu.SemaphoreType.DMA((pieces,)),
         ],
-    )(asked, me, slab)
+    )(asked, me, *[array for array, _, _, _ in sources])
 
 
 def departures_kernel(
-    slab, mirror, near, far_low, far_high, slot_of, win_of, request, me, weights, observed, used_t, inv_error,
-    kept_rows, low,
+    slab, mirror, near, far_high, slot_of, win_of, request, me, weights, observed, used_t, inv_error,
+    kept, low,
 ):
     groups, slots, cells = weights.shape
     levels = observed.shape[2]
-    windows = kept_rows.shape[0]
+    windows = kept.shape[0]
     half = windows // 2
-    n_near, n_low, n_high = len(near), len(far_low), len(far_high)
+    n_near, n_high = len(near), len(far_high)
     opposite = windows - 2
-    n_sems = 2 * GCAP + n_near + n_low + n_high
+    n_sems = 2 * GCAP + 2 * n_near + n_high
 
     def body(slot_ref, win_ref, request_ref, me_ref, w_ref, y_ref, u_ref, inv_ref, kept_ref, slab_ref, mirror_ref, *refs):
         near_refs = refs[:n_near]
-        low_refs = refs[n_near:n_near + n_low]
-        high_refs = refs[n_near + n_low:n_near + n_low + n_high]
-        out_ref, sum_ref, x_ref, sems = refs[n_near + n_low + n_high:]
+        high_refs = refs[n_near:n_near + n_high]
+        out_ref, sum_ref, x_ref, sems = refs[n_near + n_high:]
         step = pl.program_id(0)
 
         @pl.when(step == 0)
@@ -127,13 +134,13 @@
                 add(slab_ref.at[request_ref[me_ref[0], k]], x_ref.at[k])
                 add(mirror_ref.at[request_ref[me_ref[0], GCAP + k]], x_ref.at[opposite * GCAP + k, pl.ds(0, low)])
             for j in range(1, half):
-                add(near_refs[j - 1], x_ref.at[pl.ds(j * GCAP, GCAP)])
-                add(low_refs[j - 1], x_ref.at[pl.ds((j ^ opposite) * GCAP, GCAP), pl.ds(0, low)])
+                add(near_refs[j - 1].at[:, pl.ds(0, cells)], x_ref.at[pl.ds(j * GCAP, GCAP)])
+                add(near_refs[j - 1].at[:, pl.ds(cells, low)], x_ref.at[pl.ds((j ^ opposite) * GCAP, GCAP), pl.ds(0, low)])
             for j in range(half, windows):
                 add(high_refs[j - half], x_ref.at[pl.ds(j * GCAP, GCAP), pl.ds(low, cells - low)])
             sum_ref[0] = jnp.zeros((windows, levels), jnp.float32)
             sum_ref[1] = jnp.zeros((windows, levels), jnp.float32)
-            sum_ref[2] = kept_ref[...]
+            sum_ref[2] = jnp.broadcast_to(kept_ref[...], (windows, levels))
             for copy in copies:
                 copy.wait()
 
@@ -157,9 +164,9 @@
             pl.BlockSpec((STEP, slots, levels), lambda s: (s, 0, 0)),
             pl.BlockSpec((1, slots, STEP), lambda s: (s, 0, 0)),
             pl.BlockSpec((1, levels), lambda s: (0, 0)),
-            pl.BlockSpec((windows, levels), lambda s: (0, 0)),
+            pl.BlockSpec((windows, 1), lambda s: (0, 0)),
         ]
-        + [ANY] * (2 + n_near + n_low + n_high),
+        + [ANY] * (2 + n_near + n_high),
         out_specs=[
             pl.BlockSpec((STEP, slots, levels), lambda s: (s, 0, 0)),
             pl.BlockSpec((3, windows, levels), lambda s: (0, 0, 0)),
@@ -173,18 +180,17 @@
             pltpu.SemaphoreType.DMA((n_sems,)),
         ],
     )(
-        slot_of, win_of, request, me, weights, observed, used_t, inv_error[None, :], kept_rows,
-        slab, mirror, *near, *far_low, *far_high,
+        slot_of, win_of, request, me, weights, observed, used_t, inv_error[None, :], kept,
+        slab, mirror, *near, *far_high,
     )
 
 
 def body(trajectory, weights, observed, window, block, counts, flags, inv_error):
     groups, slots, cells = weights.shape
-    levels = observed.shape[2]
     windows = lax.axis_size("tm")
     half = windows // 2
     opposite = windows - 2
-    low = cells * 5 // 8 // 16 * 16
+    low = cells * 3 // 8 // 16 * 16
     me = lax.axis_index("tm").reshape(1)
     slab = trajectory[0]
 
@@ -196,23 +202,19 @@
 
     far = tuple(range(half, windows))
     close = tuple(range(1, half))
-    sent = gather_rows(asked, me, slab, far, 0, low, cells - low)
+    sent = gather_rows(asked, me, ((slab, 0, low, cells - low),), far)
     far_high = [swap(part, "tm", j) for j, part in zip(far, sent)]
-    sent = gather_rows(asked, me, slab, close, 0, 0, cells)
+    sent = gather_rows(asked, me, ((slab, 0, 0, cells), (mirror, GCAP, 0, low)), close)
     near = [swap(part, "tm", j) for j, part in zip(close, sent)]
-    sent = gather_rows(asked, me, mirror, close, GCAP, 0, low)
-    far_low = [swap(part, "tm", j) for j, part in zip(close, sent)]
 
     slot_ids = lax.broadcasted_iota(jnp.int32, (groups, slots), 1)
     used = jnp.where(slot_ids < counts[:, None], flags, 0).astype(jnp.float32)
     used_t = used.reshape(groups // STEP, STEP, slots).transpose(0, 2, 1)
     member = win_of[None, :] == jnp.arange(windows, dtype=jnp.int32)[:, None]
-    kept = jnp.sum(jnp.where(member, jnp.sum(used, 1)[None, :], 0.0), 1)
-    kept_rows = jnp.broadcast_to(kept[:, None], (windows, levels))
-
+    kept = jnp.sum(jnp.where(member, jnp.sum(used, 1)[None, :], 0.0), 1, keepdims=True)
     departures, sums = departures_kernel(
-        slab, mirror, near, far_low, far_high, slot_of, win_of, request, me, weights, observed,
-        used_t, inv_error, kept_rows, low,
+        slab, mirror, near, far_high, slot_of, win_of, request, me, weights, observed,
+        used_t, inv_error, kept, low,
     )
     for axis in ("obs", "tm"):
         bits = 1

time: 99.7 us -> 91.7 us (0.920)
  blocking collectives: 27.2 us -> 15.8 us
  waiting for transfers between devices: 28.1 us -> 34.2 us
  Pallas kernels: 15.7 us -> 13.7 us
  starting transfers between devices: 22.8 us -> 20.9 us
  local copies, waits for them, and re-layouts: 2.71 us -> 4.03 us
    all_to_all x1, blocking collectives: 27.2 us -> 15.8 us  [body(): lax.all_to_all(request[:, None], 'tm', split_axis=0, concat_axis=0, tiled...]
    ppermute x16 -> x13, waiting for transfers between devices: 28.1 us -> 34.2 us  [swap(): return lax.ppermute(x, axis, [(i, i ^ bits) for i in range(size)])]
    pallas_call x3 -> x2, Pallas kernels: 7.73 us -> 5.72 us  [gather_rows(): pl.pallas_call(body, in_specs=[SMEM, SMEM] + [ANY] * count, out_specs=[AN...]
    ppermute x16 -> x13, starting transfers between devices: 22.8 us -> 20.9 us  [swap(): return lax.ppermute(x, axis, [(i, i ^ bits) for i in range(size)])]
    unnamed x28 -> x22, local copies, waits for them, and re-layouts: 0.06 us -> 1.48 us
  transfers between devices with their start and end apart: 16 -> 13, of which waited for: 9 -> 10; matrix products, arithmetic and copies ran while one was open for 1% -> 2% of each run, Pallas kernels for 10% -> 8%
where the time goes in v2:
time: 91.7 us; the launch traced here: 91.1 us
  waiting for transfers between devices  34.2 us (37%)
  starting transfers between devices  20.9 us (23%)
  blocking collectives  15.8 us (17%)
  Pallas kernels  13.7 us (15%)
  local copies, waits for them, and re-layouts  4.03 us (4%)
  other arithmetic  1.62 us (2%)
    ppermute x13, waiting for transfers between devices, swap(): return lax.ppermute(x, axis, [(i, i ^ bits) for i in range(size)])  34.2 us
    ppermute x13, starting transfers between devices, swap(): return lax.ppermute(x, axis, [(i, i ^ bits) for i in range(size)])  20.9 us
    all_to_all x1, blocking collectives, body(): lax.all_to_all(request[:, None], 'tm', split_axis=0, concat_axis=0, tiled...  15.8 us
    pallas_call x1, Pallas kernels, departures_kernel(): pl.pallas_call(body, grid=(groups // STEP,), in_specs=[SMEM] * 4 + [pl.Bl...  6.14 us
    pallas_call x2, Pallas kernels, gather_rows(): pl.pallas_call(body, in_specs=[SMEM, SMEM] + [ANY] * count, out_specs=[AN...  5.72 us
  transfers between devices with their start and end apart: 13, of which 10 were waited for; matrix products, arithmetic and copies ran while one was open for 2% of the time, Pallas kernels for 8%

profile of v2, /device:TPU:0, one launch (start us, length us, event | category | flops | bytes accessed | tf_op | source)
XLA Modules:
  0.0 91.1 jit_solution(5935743933985083845)
XLA Ops:
  1.7 5.1 %collective-permute-start = (bf16[16,96,128]{2,1,0:T(8,128)(2,1)S(1)}, bf16[16,96,128]{2,1,0:T(8,128)(2,1)S(1)}, u32[]{:S(2)}, u32[]{:S(2)}) collective-permute-start(bf16[16,96,128]{2,1,0:T(8,128)(2,1)S(1)} %slice.17), channel_id=1, source_target_pairs={{0,24},{4,28},{8,16},{12,20},{16,8},{20,12},{24,0},{28,4},{1,25},{... | collective-permute-start | bytes 1179656 | tf_op jit(solution)/shard_map/ppermute | solution.py:19
  6.9 1.8 %shard_map.103 = (s32[8,8]{1,0:T(8,128)}, s32[32]{0:T(128)}) custom-call(s32[32]{0:T(128)} %bitcast.24, s32[32]{0:T(128)} %block_ref.1, s32[1]{0:T(128)} %bitcast.1.me_ref), custom_call_target="tpu_custom_call" | custom-call | tf_op jit(solution)/shard_map/pallas_call | solution.py:47
  8.7 15.8 %all_to_all.5 = s32[8,1,8]{2,1,0:T(1,128)} all-to-all(s32[8,1,8]{2,1,0:T(1,128)} %bitcast.23), channel_id=1, replica_groups=mesh['tm'=8,'obs'=4] {'tm'}, dimensions={0} | all-to-all | bytes 512 | tf_op jit(solution)/shard_map/all_to_all | solution.py:201
  24.5 2.7 %shard_map.105 = (bf16[4,160,128]{2,1,0:T(8,128)(2,1)}, bf16[4,160,128]{2,1,0:T(8,128)(2,1)}, bf16[4,160,128]{2,1,0:T(8,128)(2,1)}, bf16[4,160,128]{2,1,0:T(8,128)(2,1)}) custom-call(s32[8,8]{1,0:T(8,128)} %bitcast.21, s32[1]{0:T(128)} %bitcast.1.me_ref, bf16[16,256,128]{2,1,0:T(8,128)(2,1)} %bitcast.17), custom_call_target="tpu_custom_call" | custom-call | tf_op jit(solution)/shard_map/pallas_call | solution.py:93
  27.2 1.7 %collective-permute-start.4 = (bf16[4,160,128]{2,1,0:T(8,128)(2,1)}, bf16[4,160,128]{2,1,0:T(8,128)(2,1)S(1)}, u32[]{:S(2)}, u32[]{:S(2)}) collective-permute-start(bf16[4,160,128]{2,1,0:T(8,128)(2,1)} %get-tuple-element.19), channel_id=1, source_target_pairs={{0,16},{4,20},{8,24},{12,28},{16,0},{20,4},{24,8},{28,12},{1,17},{... | collective-permute-start | bytes 491528 | tf_op jit(solution)/shard_map/ppermute | solution.py:19
  28.9 1.5 %collective-permute-start.5 = (bf16[4,160,128]{2,1,0:T(8,128)(2,1)}, bf16[4,160,128]{2,1,0:T(8,128)(2,1)S(1)}, u32[]{:S(2)}, u32[]{:S(2)}) collective-permute-start(bf16[4,160,128]{2,1,0:T(8,128)(2,1)} %get-tuple-element.20), channel_id=1, source_target_pairs={{0,20},{4,16},{8,28},{12,24},{16,4},{20,0},{24,12},{28,8},{1,21},{... | collective-permute-start | bytes 491528 | tf_op jit(solution)/shard_map/ppermute | solution.py:19
  31.2 3.0 %shard_map.104 = (bf16[4,352,128]{2,1,0:T(8,128)(2,1)}, bf16[4,352,128]{2,1,0:T(8,128)(2,1)}, bf16[4,352,128]{2,1,0:T(8,128)(2,1)}) custom-call(s32[8,8]{1,0:T(8,128)} %bitcast.22, s32[1]{0:T(128)} %bitcast.1.me_ref, bf16[16,256,128]{2,1,0:T(8,128)(2,1)} %bitcast.18, bf16[16,96,128]{2,1,0:T(8,128)(2,1)} %copy-done), custom_call_target="tpu_custom_call" | custom-call | tf_op jit(solution)/shard_map/pallas_call | solution.py:93
  34.2 1.2 %collective-permute-start.1 = (bf16[4,352,128]{2,1,0:T(8,128)(2,1)}, bf16[4,352,128]{2,1,0:T(8,128)(2,1)S(1)}, u32[]{:S(2)}, u32[]{:S(2)}) collective-permute-start(bf16[4,352,128]{2,1,0:T(8,128)(2,1)} %get-tuple-element.16), channel_id=1, source_target_pairs={{0,4},{4,0},{8,12},{12,8},{16,20},{20,16},{24,28},{28,24},{1,5},{5... | collective-permute-start | bytes 1081352 | tf_op jit(solution)/shard_map/ppermute | solution.py:19
  36.1 1.7 %collective-permute-start.3 = (bf16[4,352,128]{2,1,0:T(8,128)(2,1)}, bf16[4,352,128]{2,1,0:T(8,128)(2,1)S(1)}, u32[]{:S(2)}, u32[]{:S(2)}) collective-permute-start(bf16[4,352,128]{2,1,0:T(8,128)(2,1)} %get-tuple-element.18), channel_id=1, source_target_pairs={{0,12},{4,8},{8,4},{12,0},{16,28},{20,24},{24,20},{28,16},{1,13},{... | collective-permute-start | bytes 1081352 | tf_op jit(solution)/shard_map/ppermute | solution.py:19
  38.8 2.0 %collective-permute-done.4.refs_3_ = bf16[4,160,128]{2,1,0:T(8,128)(2,1)S(1)} collective-permute-done((bf16[4,160,128]{2,1,0:T(8,128)(2,1)}, bf16[4,160,128]{2,1,0:T(8,128)(2,1)S(1)}, u32[]{:S(2)}, u32[]{:S(2)}) %collective-permute-start.4) | collective-permute-done | bytes 163872 | tf_op jit(solution)/shard_map/ppermute | solution.py:19
  40.8 2.2 %collective-permute-start.6 = (bf16[4,160,128]{2,1,0:T(8,128)(2,1)}, bf16[4,160,128]{2,1,0:T(8,128)(2,1)S(1)}, u32[]{:S(2)}, u32[]{:S(2)}) collective-permute-start(bf16[4,160,128]{2,1,0:T(8,128)(2,1)} %get-tuple-element.21), channel_id=1, source_target_pairs={{0,24},{4,28},{8,16},{12,20},{16,8},{20,12},{24,0},{28,4},{1,25},{... | collective-permute-start | bytes 491528 | tf_op jit(solution)/shard_map/ppermute | solution.py:19
  43.0 1.5 %collective-permute-done.5.refs_4_ = bf16[4,160,128]{2,1,0:T(8,128)(2,1)S(1)} collective-permute-done((bf16[4,160,128]{2,1,0:T(8,128)(2,1)}, bf16[4,160,128]{2,1,0:T(8,128)(2,1)S(1)}, u32[]{:S(2)}, u32[]{:S(2)}) %collective-permute-start.5) | collective-permute-done | bytes 163872 | tf_op jit(solution)/shard_map/ppermute | solution.py:19
  44.5 2.9 %collective-permute-start.7 = (bf16[4,160,128]{2,1,0:T(8,128)(2,1)}, bf16[4,160,128]{2,1,0:T(8,128)(2,1)S(1)}, u32[]{:S(2)}, u32[]{:S(2)}) collective-permute-start(bf16[4,160,128]{2,1,0:T(8,128)(2,1)} %get-tuple-element.22), channel_id=1, source_target_pairs={{0,28},{4,24},{8,20},{12,16},{16,12},{20,8},{24,4},{28,0},{1,29},{... | collective-permute-start | bytes 491528 | tf_op jit(solution)/shard_map/ppermute | solution.py:19
  48.4 10.0 %collective-permute-done.6.refs_5_ = bf16[4,160,128]{2,1,0:T(8,128)(2,1)S(1)} collective-permute-done((bf16[4,160,128]{2,1,0:T(8,128)(2,1)}, bf16[4,160,128]{2,1,0:T(8,128)(2,1)S(1)}, u32[]{:S(2)}, u32[]{:S(2)}) %collective-permute-start.6) | collective-permute-done | bytes 163872 | tf_op jit(solution)/shard_map/ppermute | solution.py:19
  58.3 2.8 %collective-permute-done.7.refs_6_ = bf16[4,160,128]{2,1,0:T(8,128)(2,1)S(1)} collective-permute-done((bf16[4,160,128]{2,1,0:T(8,128)(2,1)}, bf16[4,160,128]{2,1,0:T(8,128)(2,1)S(1)}, u32[]{:S(2)}, u32[]{:S(2)}) %collective-permute-start.7) | collective-permute-done | bytes 163872 | tf_op jit(solution)/shard_map/ppermute | solution.py:19
  61.2 4.6 %collective-permute-done.3.refs_2_ = bf16[4,352,128]{2,1,0:T(8,128)(2,1)S(1)} collective-permute-done((bf16[4,352,128]{2,1,0:T(8,128)(2,1)}, bf16[4,352,128]{2,1,0:T(8,128)(2,1)S(1)}, u32[]{:S(2)}, u32[]{:S(2)}) %collective-permute-start.3) | collective-permute-done | bytes 360480 | tf_op jit(solution)/shard_map/ppermute | solution.py:19
  66.6 6.1 %shard_map.106 = (bf16[32,128,128]{2,1,0:T(8,128)(2,1)}, f32[3,8,128]{2,1,0:T(8,128)}) custom-call(s32[32]{0:T(128)} %get-tuple-element.14.slot_ref, s32[32]{0:T(128)} %bitcast.25, s32[8,8]{1,0:T(8,128)} %get-tuple-element.15.request_ref, s32[1]{0:T(128)} %bitcast.1.me_ref, bf16[32,128,256]{2,1,0:T(8,128)(2,1)} %w_ref.1, bf16[32,128,128]{2,1,0:T(8,128)(2,1)} %y_ref.1, ...), custom_call_target="tpu_custom_call" | custom-call | tf_op jit(solution)/shard_map/pallas_call | solution.py:158
  72.8 1.4 %collective-permute-done.8 = f32[3,8,128]{2,1,0:T(8,128)S(1)} collective-permute-done((f32[3,8,128]{2,1,0:T(8,128)}, f32[3,8,128]{2,1,0:T(8,128)S(1)}, u32[]{:S(2)}, u32[]{:S(2)}) %collective-permute-start.8) | collective-permute-done | bytes 12320 | tf_op jit(solution)/shard_map/ppermute | solution.py:19
  74.9 1.6 %collective-permute-start.9 = (f32[3,8,128]{2,1,0:T(8,128)S(1)}, f32[3,8,128]{2,1,0:T(8,128)S(1)}, u32[]{:S(2)}, u32[]{:S(2)}) collective-permute-start(f32[3,8,128]{2,1,0:T(8,128)S(1)} %add.35), channel_id=1, source_target_pairs={{0,2},{1,3},{2,0},{3,1},{4,6},{5,7},{6,4},{7,5},{8,10},{9,11},{10,... | collective-permute-start | bytes 36872 | tf_op jit(solution)/shard_map/ppermute | solution.py:19
  76.5 2.1 %collective-permute-done.9 = f32[3,8,128]{2,1,0:T(8,128)S(1)} collective-permute-done((f32[3,8,128]{2,1,0:T(8,128)S(1)}, f32[3,8,128]{2,1,0:T(8,128)S(1)}, u32[]{:S(2)}, u32[]{:S(2)}) %collective-permute-start.9) | collective-permute-done | bytes 12320 | tf_op jit(solution)/shard_map/ppermute | solution.py:19
  78.6 1.5 %collective-permute-start.10 = (f32[3,8,128]{2,1,0:T(8,128)S(1)}, f32[3,8,128]{2,1,0:T(8,128)S(1)}, u32[]{:S(2)}, u32[]{:S(2)}) collective-permute-start(f32[3,8,128]{2,1,0:T(8,128)S(1)} %add.36), channel_id=1, source_target_pairs={{0,4},{4,0},{8,12},{12,8},{16,20},{20,16},{24,28},{28,24},{1,5},{5... | collective-permute-start | bytes 36872 | tf_op jit(solution)/shard_map/ppermute | solution.py:19
  80.0 2.2 %collective-permute-done.10 = f32[3,8,128]{2,1,0:T(8,128)S(1)} collective-permute-done((f32[3,8,128]{2,1,0:T(8,128)S(1)}, f32[3,8,128]{2,1,0:T(8,128)S(1)}, u32[]{:S(2)}, u32[]{:S(2)}) %collective-permute-start.10) | collective-permute-done | bytes 12320 | tf_op jit(solution)/shard_map/ppermute | solution.py:19
  82.3 3.7 %collective-permute-done.11 = f32[3,8,128]{2,1,0:T(8,128)S(1)} collective-permute-done((f32[3,8,128]{2,1,0:T(8,128)S(1)}, f32[3,8,128]{2,1,0:T(8,128)S(1)}, u32[]{:S(2)}, u32[]{:S(2)}) %collective-permute-start.11) | collective-permute-done | bytes 12320 | tf_op jit(solution)/shard_map/ppermute | solution.py:19
  86.7 3.8 %collective-permute-done.12 = f32[3,8,128]{2,1,0:T(8,128)S(1)} collective-permute-done((f32[3,8,128]{2,1,0:T(8,128)S(1)}, f32[3,8,128]{2,1,0:T(8,128)S(1)}, u32[]{:S(2)}, u32[]{:S(2)}) %collective-permute-start.12) | collective-permute-done | bytes 12320 | tf_op jit(solution)/shard_map/ppermute | solution.py:19
  (41 shorter events, 7.1 us)
Async XLA Ops:
  0.6 37.4 %copy-start.10 = (s32[32,1]{0,1:T(1,128)S(1)}, s32[32,1]{0,1:T(1,128)}, u32[]{:S(2)}) copy-start(s32[32,1]{0,1:T(1,128)} %param.11) | copy-start | bytes 388
  0.6 37.2 %copy-start.9 = (s32[32]{0:T(128)S(1)}, s32[32]{0:T(128)}, u32[]{:S(2)}) copy-start(s32[32]{0:T(128)} %param.13) | copy-start | bytes 388
  0.7 37.2 %copy-start.8 = (s32[32,128]{1,0:T(8,128)S(1)}, s32[32,128]{1,0:T(8,128)}, u32[]{:S(2)}) copy-start(s32[32,128]{1,0:T(8,128)} %param.14) | copy-start | bytes 49156
  1.7 28.7 %collective-permute-start = (bf16[16,96,128]{2,1,0:T(8,128)(2,1)S(1)}, bf16[16,96,128]{2,1,0:T(8,128)(2,1)S(1)}, u32[]{:S(2)}, u32[]{:S(2)}) collective-permute-start(bf16[16,96,128]{2,1,0:T(8,128)(2,1)S(1)} %slice.17), channel_id=1, source_target_pairs={{0,24},{4,28},{8,16},{12,20},{16,8},{20,12},{24,0},{28,4},{1,25},{... | collective-permute-start | bytes 1179656 | tf_op jit(solution)/shard_map/ppermute | solution.py:19
  27.2 13.6 %collective-permute-start.4 = (bf16[4,160,128]{2,1,0:T(8,128)(2,1)}, bf16[4,160,128]{2,1,0:T(8,128)(2,1)S(1)}, u32[]{:S(2)}, u32[]{:S(2)}) collective-permute-start(bf16[4,160,128]{2,1,0:T(8,128)(2,1)} %get-tuple-element.19), channel_id=1, source_target_pairs={{0,16},{4,20},{8,24},{12,28},{16,0},{20,4},{24,8},{28,12},{1,17},{... | collective-permute-start | bytes 491528 | tf_op jit(solution)/shard_map/ppermute | solution.py:19
  28.9 15.6 %collective-permute-start.5 = (bf16[4,160,128]{2,1,0:T(8,128)(2,1)}, bf16[4,160,128]{2,1,0:T(8,128)(2,1)S(1)}, u32[]{:S(2)}, u32[]{:S(2)}) collective-permute-start(bf16[4,160,128]{2,1,0:T(8,128)(2,1)} %get-tuple-element.20), channel_id=1, source_target_pairs={{0,20},{4,16},{8,28},{12,24},{16,4},{20,0},{24,12},{28,8},{1,21},{... | collective-permute-start | bytes 491528 | tf_op jit(solution)/shard_map/ppermute | solution.py:19
  30.4 0.7 copy-start
  34.2 26.9 %collective-permute-start.1 = (bf16[4,352,128]{2,1,0:T(8,128)(2,1)}, bf16[4,352,128]{2,1,0:T(8,128)(2,1)S(1)}, u32[]{:S(2)}, u32[]{:S(2)}) collective-permute-start(bf16[4,352,128]{2,1,0:T(8,128)(2,1)} %get-tuple-element.16), channel_id=1, source_target_pairs={{0,4},{4,0},{8,12},{12,8},{16,20},{20,16},{24,28},{28,24},{1,5},{5... | collective-permute-start | bytes 1081352 | tf_op jit(solution)/shard_map/ppermute | solution.py:19
  35.4 25.7 %collective-permute-start.2 = (bf16[4,352,128]{2,1,0:T(8,128)(2,1)}, bf16[4,352,128]{2,1,0:T(8,128)(2,1)S(1)}, u32[]{:S(2)}, u32[]{:S(2)}) collective-permute-start(bf16[4,352,128]{2,1,0:T(8,128)(2,1)} %get-tuple-element.17), channel_id=1, source_target_pairs={{0,8},{4,12},{8,0},{12,4},{16,24},{20,28},{24,16},{28,20},{1,9},{5... | collective-permute-start | bytes 1081352 | tf_op jit(solution)/shard_map/ppermute | solution.py:19
  36.1 29.7 %collective-permute-start.3 = (bf16[4,352,128]{2,1,0:T(8,128)(2,1)}, bf16[4,352,128]{2,1,0:T(8,128)(2,1)S(1)}, u32[]{:S(2)}, u32[]{:S(2)}) collective-permute-start(bf16[4,352,128]{2,1,0:T(8,128)(2,1)} %get-tuple-element.18), channel_id=1, source_target_pairs={{0,12},{4,8},{8,4},{12,0},{16,28},{20,24},{24,20},{28,16},{1,13},{... | collective-permute-start | bytes 1081352 | tf_op jit(solution)/shard_map/ppermute | solution.py:19
  40.8 25.0 %copy-start.4 = (bf16[4,160,128]{2,1,0:T(8,128)(2,1)}, bf16[4,160,128]{2,1,0:T(8,128)(2,1)S(1)}, u32[]{:S(2)}) copy-start(bf16[4,160,128]{2,1,0:T(8,128)(2,1)S(1)} %collective-permute-done.4.refs_3_) | copy-start | bytes 491524
  40.8 17.5 %collective-permute-start.6 = (bf16[4,160,128]{2,1,0:T(8,128)(2,1)}, bf16[4,160,128]{2,1,0:T(8,128)(2,1)S(1)}, u32[]{:S(2)}, u32[]{:S(2)}) collective-permute-start(bf16[4,160,128]{2,1,0:T(8,128)(2,1)} %get-tuple-element.21), channel_id=1, source_target_pairs={{0,24},{4,28},{8,16},{12,20},{16,8},{20,12},{24,0},{28,4},{1,25},{... | collective-permute-start | bytes 491528 | tf_op jit(solution)/shard_map/ppermute | solution.py:19
  44.5 21.3 %copy-start.5 = (bf16[4,160,128]{2,1,0:T(8,128)(2,1)}, bf16[4,160,128]{2,1,0:T(8,128)(2,1)S(1)}, u32[]{:S(2)}) copy-start(bf16[4,160,128]{2,1,0:T(8,128)(2,1)S(1)} %collective-permute-done.5.refs_4_) | copy-start | bytes 491524
  44.5 16.7 %collective-permute-start.7 = (bf16[4,160,128]{2,1,0:T(8,128)(2,1)}, bf16[4,160,128]{2,1,0:T(8,128)(2,1)S(1)}, u32[]{:S(2)}, u32[]{:S(2)}) collective-permute-start(bf16[4,160,128]{2,1,0:T(8,128)(2,1)} %get-tuple-element.22), channel_id=1, source_target_pairs={{0,28},{4,24},{8,20},{12,16},{16,12},{20,8},{24,4},{28,0},{1,29},{... | collective-permute-start | bytes 491528 | tf_op jit(solution)/shard_map/ppermute | solution.py:19
  58.3 7.5 %copy-start.6 = (bf16[4,160,128]{2,1,0:T(8,128)(2,1)}, bf16[4,160,128]{2,1,0:T(8,128)(2,1)S(1)}, u32[]{:S(2)}) copy-start(bf16[4,160,128]{2,1,0:T(8,128)(2,1)S(1)} %collective-permute-done.6.refs_5_) | copy-start | bytes 491524
  61.2 4.7 %copy-start.7 = (bf16[4,160,128]{2,1,0:T(8,128)(2,1)}, bf16[4,160,128]{2,1,0:T(8,128)(2,1)S(1)}, u32[]{:S(2)}) copy-start(bf16[4,160,128]{2,1,0:T(8,128)(2,1)S(1)} %collective-permute-done.7.refs_6_) | copy-start | bytes 491524
  61.2 4.7 %copy-start.1 = (bf16[4,352,128]{2,1,0:T(8,128)(2,1)}, bf16[4,352,128]{2,1,0:T(8,128)(2,1)S(1)}, u32[]{:S(2)}) copy-start(bf16[4,352,128]{2,1,0:T(8,128)(2,1)S(1)} %collective-permute-done.1.refs_0_) | copy-start | bytes 1081348
  61.2 4.7 %copy-start.2 = (bf16[4,352,128]{2,1,0:T(8,128)(2,1)}, bf16[4,352,128]{2,1,0:T(8,128)(2,1)S(1)}, u32[]{:S(2)}) copy-start(bf16[4,352,128]{2,1,0:T(8,128)(2,1)S(1)} %collective-permute-done.2.refs_1_) | copy-start | bytes 1081348
  65.8 0.7 copy-start.3
  72.7 1.5 %collective-permute-start.8 = (f32[3,8,128]{2,1,0:T(8,128)}, f32[3,8,128]{2,1,0:T(8,128)S(1)}, u32[]{:S(2)}, u32[]{:S(2)}) collective-permute-start(f32[3,8,128]{2,1,0:T(8,128)} %get-tuple-element.24), channel_id=1, source_target_pairs={{0,1},{1,0},{2,3},{3,2},{4,5},{5,4},{6,7},{7,6},{8,9},{9,8},{10,11... | collective-permute-start | bytes 36872 | tf_op jit(solution)/shard_map/ppermute | solution.py:19
  74.9 3.7 %collective-permute-start.9 = (f32[3,8,128]{2,1,0:T(8,128)S(1)}, f32[3,8,128]{2,1,0:T(8,128)S(1)}, u32[]{:S(2)}, u32[]{:S(2)}) collective-permute-start(f32[3,8,128]{2,1,0:T(8,128)S(1)} %add.35), channel_id=1, source_target_pairs={{0,2},{1,3},{2,0},{3,1},{4,6},{5,7},{6,4},{7,5},{8,10},{9,11},{10,... | collective-permute-start | bytes 36872 | tf_op jit(solution)/shard_map/ppermute | solution.py:19
  78.6 3.7 %collective-permute-start.10 = (f32[3,8,128]{2,1,0:T(8,128)S(1)}, f32[3,8,128]{2,1,0:T(8,128)S(1)}, u32[]{:S(2)}, u32[]{:S(2)}) collective-permute-start(f32[3,8,128]{2,1,0:T(8,128)S(1)} %add.36), channel_id=1, source_target_pairs={{0,4},{4,0},{8,12},{12,8},{16,20},{20,16},{24,28},{28,24},{1,5},{5... | collective-permute-start | bytes 36872 | tf_op jit(solution)/shard_map/ppermute | solution.py:19
  82.3 3.7 %collective-permute-start.11 = (f32[3,8,128]{2,1,0:T(8,128)S(1)}, f32[3,8,128]{2,1,0:T(8,128)S(1)}, u32[]{:S(2)}, u32[]{:S(2)}) collective-permute-start(f32[3,8,128]{2,1,0:T(8,128)S(1)} %add.37), channel_id=1, source_target_pairs={{0,8},{4,12},{8,0},{12,4},{16,24},{20,28},{24,16},{28,20},{1,9},{5... | collective-permute-start | bytes 36872 | tf_op jit(solution)/shard_map/ppermute | solution.py:19
  86.0 4.6 %collective-permute-start.12 = (f32[3,8,128]{2,1,0:T(8,128)S(1)}, f32[3,8,128]{2,1,0:T(8,128)S(1)}, u32[]{:S(2)}, u32[]{:S(2)}) collective-permute-start(f32[3,8,128]{2,1,0:T(8,128)S(1)} %add.38), channel_id=1, source_target_pairs={{0,16},{4,20},{8,24},{12,28},{16,0},{20,4},{24,8},{28,12},{1,17},{... | collective-permute-start | bytes 36872 | tf_op jit(solution)/shard_map/ppermute | solution.py:19
